TPU v7x, 32 devices: a whole 2x2x4 slice. The times are simulated.
32 devices in a mesh: mesh: 2 (over core), dom: 16 (over z, y, x).
Axes of the slice: x: 2, y: 2, z: 4, core: 2. Of those that a mesh axis runs over, the one named last changes fastest.
Arguments:
- donor_fields: float32 [5, 512, 4096], P(None, None, ('mesh', 'dom')), may hold values from -6 to 6
- interp_weights: float32 [3, 8, 65536], P(None, None, ('mesh', 'dom')), may hold values from -1 to 1, as said below
- donor_owner: int32 [65536, 1], P(('mesh', 'dom')), may hold values from 0 to 15, as said below
- donor_element: int32 [65536], P(('mesh', 'dom')), may hold values from 0 to 127
- geometry: float32 [4, 4096], P(None, ('mesh', 'dom')), may hold values from 0.25 to 4
- wall_flag: int32 [2, 256], P(None, ('mesh', 'dom')), may hold values 0 or 1
- forcing: float32 [512, 4096], P(None, ('mesh', 'dom')), may hold values from -6 to 6
Outputs:
- velocity: float32 [512, 4096], P(None, ('mesh', 'dom'))
- residual: float32 [512, 4096], P(None, ('mesh', 'dom'))
- interface_values: float32 [5, 65536], P(None, ('mesh', 'dom'))
Inputs may be any that keep to these rules, and one draw needn't show every extreme that they name: `interp_weights`: for each receptor and direction, the 8 entries are the Lagrange polynomials of the order-7 Gauss-Lobatto-Legendre points evaluated at one point of [-1, 1]. `donor_owner`: the receptors of block q of a mesh (the rows of one device) name donor dom indices from q - 2 to q + 2 only; among them one index is named exactly 1024 times and no index more often.
All inputs are finite; a program needn't handle non-finite values. No bound on the sum of `wall_flag` on one device may be relied on, other than what follows from the above.
Results may differ from a plain program's by a relative error of at most 0.00026.
Values sent between devices are 32-bit elements; how exact they have to be, the bound alone decides.
A program may use at most 192 MiB of HBM per device.

v0:
```python
import functools

import jax
import jax.numpy as jnp
import numpy as np
from jax import lax
from jax.experimental import pallas as pl
from jax.experimental.pallas import tpu as pltpu
from jax.sharding import PartitionSpec as P

EX = 8
EY = 16
ITERS = 3
REACH = 2
CHUNK = 256
ORDER = (0, 7, 1, 2, 3, 4, 5, 6)
MESH = pl.DeviceIdType.MESH


def legendre_pair(values, degree):
    previous = values * 0.0 + 1.0
    current = values * 1.0
    for poly_order in range(2, degree + 1):
        previous, current = (
            current,
            ((2 * poly_order - 1) * values * current - (poly_order - 1) * previous) / poly_order,
        )
    return (current, previous)


def gll_tables():
    degree = 7
    points_count = degree + 1
    abscissae = np.cos(np.pi * np.arange(points_count) / degree)
    for newton_turn in range(80):
        top_poly, lower_poly = legendre_pair(abscissae, degree)
        abscissae = abscissae - (abscissae * top_poly - lower_poly) / (points_count * top_poly)
    abscissae = np.sort(abscissae)
    top_poly, lower_poly = legendre_pair(abscissae, degree)
    quad_weights = 2.0 / (degree * points_count * top_poly * top_poly)
    identity_mat = np.eye(points_count)
    spacing = abscissae[:, None] - abscissae[None, :] + identity_mat
    derivative = top_poly[:, None] / (top_poly[None, :] * spacing) * (1.0 - identity_mat)
    derivative[0, 0] = -degree * points_count / 4.0
    derivative[degree, degree] = degree * points_count / 4.0
    return (abscissae, derivative, quad_weights)


def kernel(
    n,
    request_ref,
    donor_hbm,
    geometry_ref,
    wall_ref,
    forcing_hbm,
    velocity_ref,
    residual_ref,
    interface_ref,
    donor_ref,
    forcing_ref,
    along_y_ref,
    along_x_ref,
    plane_ref,
    load_sem,
    split,
    asked,
    answer,
    answered,
    faces,
    halo,
    dots,
    all_dots,
    state,
    image,
    direction,
    direction_image,
    inverse,
    free,
    sharing,
    boundary,
    ask_send,
    ask_recv,
    reply_send,
    reply_recv,
    face_send,
    face_recv,
    dot_send,
    dot_recv,
):
    points, derivative, quad = gll_tables()
    stiff = (derivative.T * quad) @ derivative / quad[:, None]
    fields = donor_ref.shape[0]
    elems = donor_ref.shape[2]
    receptors = request_ref.shape[1]
    slots = 2 * REACH + 1
    mesh_id = lax.axis_index("mesh")
    slab = lax.axis_index("dom")
    other = 1 - mesh_id

    donor_load = pltpu.make_async_copy(donor_hbm, donor_ref, load_sem.at[0])
    forcing_load = pltpu.make_async_copy(forcing_hbm, forcing_ref, load_sem.at[1])
    donor_load.start()
    forcing_load.start()

    def inside(index):
        return jnp.logical_and(index >= 0, index < n)

    barrier = pltpu.get_barrier_semaphore()
    greeted = n - 1
    for step in range(1, n):
        pl.semaphore_signal(
            barrier, inc=1, device_id=(mesh_id, lax.rem(slab + step, n)), device_id_type=MESH
        )
    for shift in range(-REACH, REACH + 1):
        greeted = greeted + jnp.where(inside(slab + shift), 1, 0)

        @pl.when(inside(slab + shift))
        def _():
            pl.semaphore_signal(
                barrier, inc=1, device_id=(other, slab + shift), device_id_type=MESH
            )

    pl.semaphore_wait(barrier, greeted)

    def ask(shift):
        return pltpu.make_async_remote_copy(
            src_ref=request_ref,
            dst_ref=asked.at[shift + REACH],
            send_sem=ask_send.at[shift + REACH],
            recv_sem=ask_recv.at[shift + REACH],
            device_id=(other, lax.rem(slab + shift + n, n)),
            device_id_type=MESH,
        )

    def reply(shift):
        return pltpu.make_async_remote_copy(
            src_ref=answer.at[shift + REACH],
            dst_ref=answered.at[shift + REACH],
            send_sem=reply_send.at[shift + REACH],
            recv_sem=reply_recv.at[shift + REACH],
            device_id=(other, lax.rem(slab - shift + n, n)),
            device_id_type=MESH,
        )

    def face_copy(phase, up):
        step = 1 if up else n - 1
        return pltpu.make_async_remote_copy(
            src_ref=faces.at[phase, 1 if up else 0],
            dst_ref=halo.at[phase, 0 if up else 1],
            send_sem=face_send.at[phase, 1 if up else 0],
            recv_sem=face_recv.at[phase, 0 if up else 1],
            device_id=(mesh_id, lax.rem(slab + step, n)),
            device_id_type=MESH,
        )

    def send_faces(phase):
        @pl.when(slab < n - 1)
        def _():
            face_copy(phase, True).start()

        @pl.when(slab > 0)
        def _():
            face_copy(phase, False).start()

    def wait_faces(phase):
        @pl.when(slab > 0)
        def _():
            face_copy(phase, True).wait_recv()

        @pl.when(slab < n - 1)
        def _():
            face_copy(phase, False).wait_recv()

        @pl.when(slab < n - 1)
        def _():
            face_copy(phase, True).wait_send()

        @pl.when(slab > 0)
        def _():
            face_copy(phase, False).wait_send()

    def dot_copy(turn, step):
        return pltpu.make_async_remote_copy(
            src_ref=dots.at[turn],
            dst_ref=all_dots.at[turn, slab],
            send_sem=dot_send.at[turn, step],
            recv_sem=dot_recv.at[turn, step],
            device_id=(mesh_id, lax.rem(slab + step, n)),
            device_id_type=MESH,
        )

    for distance in range(REACH + 1):
        for shift in sorted({distance, -distance}):

            @pl.when(inside(slab + shift))
            def _():
                ask(shift).start()

    phases = halo.shape[0]
    blank = jnp.zeros(halo.shape[2:], jnp.float32)

    @pl.when(slab == 0)
    def _():
        for phase in range(phases):
            halo[phase, 0] = blank

    @pl.when(slab == n - 1)
    def _():
        for phase in range(phases):
            halo[phase, 1] = blank

    node = lax.broadcasted_iota(jnp.int32, (8, elems), 0)
    element = lax.broadcasted_iota(jnp.int32, (8, elems), 1)
    x_index = element % EX
    y_index = element // EX % EY

    across = jnp.zeros((8, elems), jnp.float32)
    for a in range(8):
        across = jnp.where(node == a, float(quad[a]), across)
    for j in range(8):
        plane_ref[j] = across * float(quad[j])
        for m in range(8):
            along_y_ref[m, j] = jnp.full((8, elems), float(stiff[j, m]), jnp.float32)
    for step in range(8):
        turned = jnp.zeros((8, elems), jnp.float32)
        for i in range(8):
            turned = jnp.where(node == i, float(stiff[i, (i - step) % 8]), turned)
        along_x_ref[step] = turned

    def flag(condition):
        return jnp.where(condition, 1.0, 0.0)

    x_low = flag((node == 0) & (x_index > 0))
    x_high = flag((node == 7) & (x_index < EX - 1))
    y_low = flag(y_index > 0)
    y_high = flag(y_index < EY - 1)

    def plane_sum(tile):
        below = pltpu.roll(pltpu.roll(tile, 1, 1), 1, 2)
        above = pltpu.roll(pltpu.roll(tile, 7, 1), elems - 1, 2)
        tile = tile + below * x_low + above * x_high
        low = tile[0] + y_low * pltpu.roll(tile[7], EX, 1)
        high = tile[7] + y_high * pltpu.roll(tile[0], elems - EX, 1)
        return jnp.concatenate([low[None], tile[1:7], high[None]], 0)

    def weights(layer):
        return plane_ref[...] * float(quad[layer])

    g_x, g_y, g_z, g_m = [geometry_ref[d : d + 1, :] for d in range(4)]

    diag_plane = jnp.zeros((8, 8, elems), jnp.float32) + g_m
    diag_plane = diag_plane + g_x * along_x_ref[0]
    diag_plane = diag_plane + jnp.concatenate(
        [(g_y * float(stiff[j, j]) + jnp.zeros((8, elems), jnp.float32))[None] for j in range(8)], 0
    )
    for layer in ORDER:
        image[layer] = plane_sum(
            weights(layer) * (diag_plane + g_z * float(stiff[layer, layer]))
        )
    wall_low = flag(y_index == 0) * wall_ref[0:1, :]
    wall_high = flag(y_index == EY - 1) * wall_ref[1:2, :]
    nothing = jnp.zeros((6, 8, elems), jnp.float32)
    wall_plane = plane_sum(jnp.concatenate([wall_low[None], nothing, wall_high[None]], 0))
    faces[0, 0] = image[0]
    faces[0, 1] = image[7]
    faces[1, 0] = wall_plane
    faces[1, 1] = wall_plane
    send_faces(0)
    send_faces(1)

    donor_load.wait()
    donors = donor_ref[...].reshape(fields * 512, elems)
    coarse = donors.astype(jnp.bfloat16)
    split[:, :elems] = coarse
    split[:, elems:] = (donors - coarse.astype(jnp.float32)).astype(jnp.bfloat16)

    code = lax.broadcasted_iota(jnp.int32, (elems, CHUNK), 0) + slab * elems
    code = code.astype(jnp.float32)
    basis = lax.broadcasted_iota(jnp.int32, (8, CHUNK), 0)
    norms = [
        float(1.0 / np.prod([points[a] - points[b] for b in range(8) if b != a])) for a in range(8)
    ]
    scale = jnp.zeros((8, CHUNK), jnp.float32)
    for a in range(8):
        scale = jnp.where(basis == a, norms[a], scale)

    def lagrange(position):
        value = scale
        for b in range(8):
            value = value * jnp.where(basis == b, 1.0, position - float(points[b]))
        return value

    def serve(turn, carry):
        shift = ((turn + 1) // 2) * (2 * (turn % 2) - 1)

        @pl.when(inside(slab - shift))
        def _():
            ask(shift).wait_recv()

            def part(chunk, carry):
                block = asked[shift + REACH, :, pl.ds(pl.multiple_of(chunk * CHUNK, CHUNK), CHUNK)]
                chosen = jnp.where(block[3:4, :] == code, 1.0, 0.0).astype(jnp.bfloat16)
                chosen = jnp.concatenate([chosen, chosen], 0)
                w_x, w_y, w_z = [lagrange(block[d : d + 1, :]) for d in range(3)]
                found = jnp.dot(split[...], chosen, preferred_element_type=jnp.float32)
                for field in range(fields):
                    cube = found[field * 512 : (field + 1) * 512].reshape(8, 64, CHUNK)
                    total = cube[0] * w_z[0:1, :]
                    for k in range(1, 8):
                        total = total + cube[k] * w_z[k : k + 1, :]
                    total = total.reshape(8, 8, CHUNK)
                    line = total[0] * w_y[0:1, :]
                    for j in range(1, 8):
                        line = line + total[j] * w_y[j : j + 1, :]
                    answer[shift + REACH, field, pl.ds(chunk, 1), :] = jnp.sum(
                        line * w_x, axis=0, keepdims=True
                    )
                return carry

            lax.fori_loop(0, receptors // CHUNK, part, 0)
            reply(shift).start()

        return carry

    lax.fori_loop(0, slots, serve, 0)

    z_low = jnp.where(slab > 0, 2.0, 1.0)
    z_high = jnp.where(slab < n - 1, 2.0, 1.0)
    x_count = 1.0 + x_low + x_high
    y_count_low = 1.0 + y_low
    y_count_high = 1.0 + y_high
    plane_count = jnp.concatenate(
        [(x_count * y_count_low)[None]]
        + [x_count[None]] * 6
        + [(x_count * y_count_high)[None]],
        0,
    )
    mark = flag((node == 0) & (x_index == 0)) + flag((node == 7) & (x_index == EX - 1))
    wait_faces(0)
    wait_faces(1)
    image[0] = image[0] + halo[0, 0]
    image[7] = image[7] + halo[0, 1]
    for layer in range(8):
        count = plane_count
        walls = wall_plane
        if layer == 0:
            count = count * z_low
            walls = walls + halo[1, 0]
        if layer == 7:
            count = count * z_high
            walls = walls + halo[1, 1]
        open_part = 1.0 - jnp.minimum(mark * count + walls, 1.0)
        sharing[layer] = 1.0 / count
        free[layer] = open_part
        inverse[layer] = open_part / image[layer]

    interface_sum = jnp.zeros((fields, receptors // CHUNK, CHUNK), jnp.float32)
    for shift in range(-REACH, REACH + 1):

        @pl.when(jnp.logical_not(inside(slab + shift)))
        def _():
            answered[shift + REACH] = jnp.zeros(answered.shape[1:], jnp.float32)

        @pl.when(inside(slab + shift))
        def _():
            reply(shift).wait_recv()

    for shift in range(-REACH, REACH + 1):
        interface_sum = interface_sum + answered[shift + REACH]
    for chunk in range(receptors // CHUNK):
        interface_ref[:, chunk * CHUNK : (chunk + 1) * CHUNK] = interface_sum[:, chunk, :]

    rows = interface_sum[0]
    groups = CHUNK // 64
    rows = jnp.concatenate([rows[:, t * 64 : (t + 1) * 64] for t in range(groups)], 0)
    count = receptors // CHUNK
    per_side = count // 2
    row = lax.broadcasted_iota(jnp.int32, (groups * count, elems), 0)
    spot = lax.broadcasted_iota(jnp.int32, (groups * count, elems), 1)
    piece = row % count
    target = (groups * (piece % per_side) + row // count) * EX + (EX - 1) * (piece // per_side)
    placed = lax.dot_general(
        rows,
        flag(spot == target),
        (((0,), (0,)), ((), ())),
        precision=lax.Precision.HIGHEST,
        preferred_element_type=jnp.float32,
    ).reshape(8, 8, elems)
    for layer in ORDER:
        spread = jnp.concatenate(
            [(jnp.broadcast_to(placed[layer, j : j + 1, :], (8, elems)) * mark)[None] for j in range(8)],
            0,
        )
        boundary[layer] = plane_sum(spread)
        if layer == 7:
            faces[2, 0] = boundary[0]
            faces[2, 1] = boundary[7]
            send_faces(2)
    wait_faces(2)
    boundary[0] = boundary[0] + halo[2, 0]
    boundary[7] = boundary[7] + halo[2, 1]
    for layer in range(8):
        boundary[layer] = boundary[layer] * sharing[layer]

    def local_tile(source, layer):
        tile = source[layer]
        along_z = source[0] * float(stiff[layer, 0])
        for k in range(1, 8):
            along_z = along_z + source[k] * float(stiff[layer, k])
        along_y = along_y_ref[0] * tile[0:1]
        for j in range(1, 8):
            along_y = along_y + along_y_ref[j] * tile[j : j + 1]
        along_x = along_x_ref[0] * tile
        for step in range(1, 8):
            along_x = along_x + along_x_ref[step] * pltpu.roll(tile, step, 1)
        total = g_x * along_x + g_y * along_y + g_z * along_z + g_m * tile
        return weights(layer) * total

    forcing_load.wait()
    for layer in ORDER:
        loaded = weights(layer) * g_m * forcing_ref[layer] - local_tile(boundary, layer)
        residual_ref[layer] = plane_sum(loaded)
        if layer == 7:
            faces[3, 0] = residual_ref[0]
            faces[3, 1] = residual_ref[7]
            send_faces(3)
    wait_faces(3)
    residual_ref[0] = residual_ref[0] + halo[3, 0]
    residual_ref[7] = residual_ref[7] + halo[3, 1]
    for layer in range(8):
        residual_ref[layer] = residual_ref[layer] * free[layer]
        velocity_ref[layer] = boundary[layer]
        direction[layer] = jnp.zeros((8, 8, elems), jnp.float32)
        direction_image[layer] = jnp.zeros((8, 8, elems), jnp.float32)

    def iterate(turn, carry):
        norm, length = carry
        phase = turn + 4
        norm_part = jnp.zeros((8, 8, elems), jnp.float32)
        for layer in range(8):
            state[layer] = inverse[layer] * residual_ref[layer]
            norm_part = norm_part + state[layer] * residual_ref[layer] * sharing[layer]
        curve_part = jnp.zeros((8, 8, elems), jnp.float32)
        for layer in ORDER:
            tile = local_tile(state, layer)
            curve_part = curve_part + tile * state[layer]
            image[layer] = plane_sum(tile)
            if layer == 7:
                faces[phase, 0] = image[0]
                faces[phase, 1] = image[7]
                send_faces(phase)
        dots[turn, 0:1, :] = jnp.sum(jnp.sum(norm_part, axis=0), axis=0, keepdims=True)
        dots[turn, 1:2, :] = jnp.sum(jnp.sum(curve_part, axis=0), axis=0, keepdims=True)
        for step in range(1, n):
            dot_copy(turn, step).start()
        all_dots[turn, slab] = dots[turn]
        wait_faces(phase)
        image[0] = image[0] + halo[phase, 0]
        image[7] = image[7] + halo[phase, 1]
        for step in range(1, n):
            dot_copy(turn, step).wait_recv()
        sums = jnp.sum(jnp.sum(all_dots[turn], axis=0), axis=1, keepdims=True)
        norm_next, curvature = sums[0:1, :], sums[1:2, :]
        ratio = jnp.where(turn == 0, 0.0, norm_next / norm)
        length = norm_next / (curvature - ratio * norm_next / length)
        for layer in range(8):
            toward = state[layer] + ratio * direction[layer]
            toward_image = free[layer] * image[layer] + ratio * direction_image[layer]
            direction[layer] = toward
            direction_image[layer] = toward_image
            velocity_ref[layer] = velocity_ref[layer] + length * toward
            residual_ref[layer] = residual_ref[layer] - length * toward_image
        for step in range(1, n):
            dot_copy(turn, step).wait_send()
        return norm_next, length

    one = jnp.ones((1, 1), jnp.float32)
    lax.fori_loop(0, ITERS, iterate, (one, one))

    for shift in range(-REACH, REACH + 1):

        @pl.when(inside(slab + shift))
        def _():
            ask(shift).wait_send()

        @pl.when(inside(slab - shift))
        def _():
            reply(shift).wait_send()


def body(n, donor_fields, interp_weights, donor_owner, donor_element, geometry, wall_flag, forcing):
    points, _, _ = gll_tables()
    fields = donor_fields.shape[0]
    elems = geometry.shape[1]
    receptors = donor_element.shape[0]
    slots = 2 * REACH + 1
    nodes = jnp.asarray(points, jnp.float32)
    position = jnp.sum(interp_weights * nodes[None, :, None], axis=1)
    code = (donor_owner[:, 0] * elems + donor_element).astype(jnp.float32)
    request = jnp.concatenate([position, code[None, :]], 0)
    walls = jnp.tile(wall_flag.astype(jnp.float32), (1, elems // wall_flag.shape[1]))
    count = receptors // CHUNK
    cube = (8, 8, 8, elems)
    phases = 4 + ITERS
    vmem = pl.BlockSpec(memory_space=pltpu.VMEM)
    hbm = pl.BlockSpec(memory_space=pl.ANY)
    velocity, residual, interface = pl.pallas_call(
        functools.partial(kernel, n),
        out_shape=(
            jax.ShapeDtypeStruct(cube, jnp.float32),
            jax.ShapeDtypeStruct(cube, jnp.float32),
            jax.ShapeDtypeStruct((fields, receptors), jnp.float32),
        ),
        in_specs=[vmem, hbm, vmem, vmem, hbm],
        out_specs=(vmem, vmem, vmem),
        scratch_shapes=[
            pltpu.VMEM((fields, 512, elems), jnp.float32),
            pltpu.VMEM(cube, jnp.float32),
            pltpu.VMEM(cube, jnp.float32),
            pltpu.VMEM((8, 8, elems), jnp.float32),
            pltpu.VMEM((8, 8, elems), jnp.float32),
            pltpu.SemaphoreType.DMA((2,)),
            pltpu.VMEM((fields * 512, 2 * elems), jnp.bfloat16),
            pltpu.VMEM((slots, 4, receptors), jnp.float32),
            pltpu.VMEM((slots, fields, count, CHUNK), jnp.float32),
            pltpu.VMEM((slots, fields, count, CHUNK), jnp.float32),
            pltpu.VMEM((phases, 2, 8, 8, elems), jnp.float32),
            pltpu.VMEM((phases, 2, 8, 8, elems), jnp.float32),
            pltpu.VMEM((ITERS, 2, 128), jnp.float32),
            pltpu.VMEM((ITERS, n, 2, 128), jnp.float32),
        ]
        + [pltpu.VMEM(cube, jnp.float32)] * 8
        + [pltpu.SemaphoreType.DMA((slots,))] * 4
        + [pltpu.SemaphoreType.DMA((phases, 2))] * 2
        + [pltpu.SemaphoreType.DMA((ITERS, n))] * 2,
        compiler_params=pltpu.CompilerParams(
            collective_id=0, has_side_effects=True, vmem_limit_bytes=48 * 1024 * 1024
        ),
    )(
        request,
        donor_fields,
        geometry,
        walls,
        forcing.reshape(cube),
    )
    return (velocity.reshape(512, elems), residual.reshape(512, elems), interface)


def solution(mesh):
    in_specs = (
        P(None, None, ("mesh", "dom")),
        P(None, None, ("mesh", "dom")),
        P(("mesh", "dom"), None),
        P(("mesh", "dom")),
        P(None, ("mesh", "dom")),
        P(None, ("mesh", "dom")),
        P(None, ("mesh", "dom")),
    )
    out_specs = (P(None, ("mesh", "dom")), P(None, ("mesh", "dom")), P(None, ("mesh", "dom")))
    return jax.shard_map(
        functools.partial(body, mesh.shape["dom"]),
        mesh=mesh,
        in_specs=in_specs,
        out_specs=out_specs,
        check_vma=False,
    )
```

profile of v0, /device:TPU:0, one launch (start us, length us, event | category | flops | bytes accessed | tf_op | source)
XLA Modules:
  0.0 66.4 jit_solution(8760335562207359234)
XLA Ops:
  0.6 0.7 %convert_element_type.7 = f32[2,8]{1,0:T(2,128)S(1)} convert(s32[2,8]{1,0:T(2,128)} %param.13) | non-fusion elementwise | flops 16 | bytes 128 | tf_op jit(solution)/shard_map/convert_element_type | solution.py:501
  1.3 0.7 %broadcast_multiply_fusion = s32[2048,1]{0,1:T(1,128)S(1)} fusion(s32[2048,1]{0,1:T(1,128)} %param.10), kind=kLoop, calls=%fused_computation.3 | loop fusion | flops 2048 | bytes 16384 | tf_op jit(solution)/shard_map/mul | solution.py:499
  2.0 0.7 %add_convert_fusion = f32[2048]{0:T(1024)S(1)} fusion(s32[2048]{0:T(1024)S(1)} %bitcast.9, s32[2048]{0:T(1024)} %param.11), kind=kLoop, calls=%fused_computation.2 | loop fusion | flops 4096 | bytes 24576 | tf_op jit(solution)/shard_map/convert_element_type | solution.py:499
  2.7 0.1 tile.10.wall_ref
  2.8 1.1 %multiply_reduce_fusion = f32[3,2048]{1,0:T(4,128)S(1)} fusion(f32[3,8,2048]{2,1,0:T(8,128)} %param.9, f32[8]{0:T(128)} %constant.6.clone), kind=kLoop, calls=%fused_computation | loop fusion | flops 92160 | bytes 221216 | tf_op jit(solution)/shard_map/reduce_sum | solution.py:498
  3.9 0.0 copy-start
  3.9 1.3 %copy-done = f32[5,512,128]{2,1,0:T(8,128)S(1)} copy-done((f32[5,512,128]{2,1,0:T(8,128)S(1)}, f32[5,512,128]{2,1,0:T(8,128)}, u32[]{:S(2)}) %copy-start) | copy-done | bytes 1310744
  5.2 0.0 copy-start.1
  5.2 0.9 %copy-done.1 = f32[512,128]{1,0:T(8,128)S(1)} copy-done((f32[512,128]{1,0:T(8,128)S(1)}, f32[512,128]{1,0:T(8,128)}, u32[]{:S(2)}) %copy-start.1) | copy-done | bytes 262168
  6.2 0.0 copy-start.2
  6.2 0.7 %copy-done.2 = f32[4,128]{1,0:T(4,128)S(1)} copy-done((f32[4,128]{1,0:T(4,128)S(1)}, f32[4,128]{1,0:T(4,128)}, u32[]{:S(2)}) %copy-start.2) | copy-done | bytes 2072
  6.9 57.5 %shard_map.103 = (f32[8,8,8,128]{3,2,1,0:T(8,128)S(1)}, f32[8,8,8,128]{3,2,1,0:T(8,128)S(1)}, f32[5,2048]{1,0:T(8,128)S(1)}) custom-call(f32[4,2048]{1,0:T(4,128)S(1)} %pad_maximum_fusion.request_ref, f32[5,512,128]{2,1,0:T(8,128)S(1)} %copy-done, f32[4,128]{1,0:T(4,128)S(1)} %copy-done.2, f32[2,128]{1,0:T(2,128)S(1)} %tile.10.wall_ref, ...), custom_call_target="tpu_custom_call" | custom-call | tf_op jit(solution)/shard_map/pallas_call | solution.py:507
  64.4 0.7 %copy.14 = f32[512,128]{1,0:T(8,128)} copy(f32[512,128]{1,0:T(8,128)S(1)} %bitcast.6) | data formatting | bytes 524288
  65.1 0.7 %copy.15 = f32[512,128]{1,0:T(8,128)} copy(f32[512,128]{1,0:T(8,128)S(1)} %bitcast.5) | data formatting | bytes 524288
  65.8 0.6 copy.16
  (2 shorter events, 0.0 us)
Async XLA Ops:
  3.9 1.3 %copy-start = (f32[5,512,128]{2,1,0:T(8,128)S(1)}, f32[5,512,128]{2,1,0:T(8,128)}, u32[]{:S(2)}) copy-start(f32[5,512,128]{2,1,0:T(8,128)} %donor_hbm.1) | copy-start | bytes 3932164
  5.2 0.9 %copy-start.1 = (f32[512,128]{1,0:T(8,128)S(1)}, f32[512,128]{1,0:T(8,128)}, u32[]{:S(2)}) copy-start(f32[512,128]{1,0:T(8,128)} %param.14) | copy-start | bytes 786436
  6.2 0.7 %copy-start.2 = (f32[4,128]{1,0:T(4,128)S(1)}, f32[4,128]{1,0:T(4,128)}, u32[]{:S(2)}) copy-start(f32[4,128]{1,0:T(4,128)} %geometry_ref.1) | copy-start | bytes 6148
where the time goes:
time: 66.7 us; the launch traced here: 66.4 us
  Pallas kernels  57.5 us (86%)
  local copies, waits for them, and re-layouts  5.07 us (8%)
  other arithmetic  3.17 us (5%)
    pallas_call x1, Pallas kernels, body(): pl.pallas_call(functools.partial(kernel, n), out_shape=(jax.ShapeDtypeStr...  57.5 us
    unnamed x9, local copies, waits for them, and re-layouts  4.98 us

commit v1 on v0

--- a/solution.py
+++ b/solution.py
@@ -48,16 +48,26 @@
 
 def kernel(
     n,
-    request_ref,
     donor_hbm,
-    geometry_ref,
-    wall_ref,
+    weights_hbm,
+    owner_hbm,
+    element_hbm,
+    geometry_hbm,
+    wall_hbm,
     forcing_hbm,
     velocity_ref,
     residual_ref,
     interface_ref,
     donor_ref,
     forcing_ref,
+    weights_ref,
+    owner_ref,
+    element_ref,
+    geometry_ref,
+    wall_ref,
+    position_ref,
+    request_ref,
+    moves,
     along_y_ref,
     along_x_ref,
     plane_ref,
@@ -91,16 +101,30 @@
     stiff = (derivative.T * quad) @ derivative / quad[:, None]
     fields = donor_ref.shape[0]
     elems = donor_ref.shape[2]
-    receptors = request_ref.shape[1]
+    height = owner_ref.shape[0]
+    lanes = owner_ref.shape[1]
+    receptors = height * lanes
+    room = request_ref.shape[2]
     slots = 2 * REACH + 1
     mesh_id = lax.axis_index("mesh")
     slab = lax.axis_index("dom")
     other = 1 - mesh_id
 
-    donor_load = pltpu.make_async_copy(donor_hbm, donor_ref, load_sem.at[0])
-    forcing_load = pltpu.make_async_copy(forcing_hbm, forcing_ref, load_sem.at[1])
-    donor_load.start()
-    forcing_load.start()
+    pairs = [
+        (weights_hbm, weights_ref),
+        (owner_hbm, owner_ref),
+        (element_hbm, element_ref),
+        (donor_hbm, donor_ref),
+        (geometry_hbm, geometry_ref),
+        (wall_hbm, wall_ref),
+        (forcing_hbm, forcing_ref),
+    ]
+    loads = [
+        pltpu.make_async_copy(source, target, load_sem.at[at])
+        for at, (source, target) in enumerate(pairs)
+    ]
+    for load in loads:
+        load.start()
 
     def inside(index):
         return jnp.logical_and(index >= 0, index < n)
@@ -120,11 +144,84 @@
                 barrier, inc=1, device_id=(other, slab + shift), device_id_type=MESH
             )
 
+    for load in loads[:3]:
+        load.wait()
+    depth = lax.broadcasted_iota(jnp.int32, (8, lanes), 0)
+    ladder = jnp.zeros((8, lanes), jnp.float32)
+    for a in range(8):
+        ladder = jnp.where(depth == a, float(points[a]), ladder)
+    for d in range(3):
+        for row in range(height):
+            part = weights_ref[d, :, row * lanes : (row + 1) * lanes] * ladder
+            position_ref[d, row : row + 1, :] = jnp.sum(part, axis=0, keepdims=True)
+    owner = owner_ref[...]
+    element_code = element_ref[...] * receptors
+    members = [owner == slab + shift for shift in range(-REACH, REACH + 1)]
+    tall = slots * height
+    marks = jnp.concatenate([jnp.where(m, 1.0, 0.0) for m in members], 0).astype(jnp.bfloat16)
+    before = lax.broadcasted_iota(jnp.int32, (lanes, lanes), 0)
+    after = lax.broadcasted_iota(jnp.int32, (lanes, lanes), 1)
+    upper = jnp.where(before < after, 1.0, 0.0).astype(jnp.bfloat16)
+    left = jnp.dot(marks, upper, preferred_element_type=jnp.float32).astype(jnp.bfloat16)
+    above = lax.broadcasted_iota(jnp.int32, (tall, tall), 0)
+    below = lax.broadcasted_iota(jnp.int32, (tall, tall), 1)
+    same = above // height == below // height
+    block = jnp.where(same, 1.0, 0.0).astype(jnp.bfloat16)
+    lower = jnp.where(same & (below < above), 1.0, 0.0).astype(jnp.bfloat16)
+    rank = jnp.dot(block, left, preferred_element_type=jnp.float32)
+    rank = rank + jnp.dot(lower, marks, preferred_element_type=jnp.float32)
+    rank = rank.astype(jnp.int32)
+    row_index = lax.broadcasted_iota(jnp.int32, (height, lanes), 0)
+    place = lax.broadcasted_iota(jnp.int32, (height, lanes), 1) * height + row_index
+    row_bits = height.bit_length() - 1
+    steps = receptors.bit_length() - 1
+
+    def pull(tile, step):
+        if step >= row_bits:
+            return pltpu.roll(tile, lanes - (1 << (step - row_bits)), 1)
+        jump = 1 << step
+        near = pltpu.roll(tile, height - jump, 0)
+        far = pltpu.roll(near, lanes - 1, 1)
+        return jnp.where(row_index < height - jump, near, far)
+
+    def push(tile, step):
+        if step >= row_bits:
+            return pltpu.roll(tile, 1 << (step - row_bits), 1)
+        jump = 1 << step
+        near = pltpu.roll(tile, jump, 0)
+        far = pltpu.roll(near, 1, 1)
+        return jnp.where(row_index >= jump, near, far)
+
+    words = []
+    comps = []
+    start = [position_ref[d] for d in range(3)]
+    for slot in range(slots):
+        shift = place - rank[slot * height : (slot + 1) * height]
+        words.append(jnp.where(members[slot], element_code + shift, 0))
+        comps.append(list(start))
+    for step in range(steps):
+        for slot in range(slots):
+            word = words[slot]
+            moving = word & (1 << step)
+            moves[step, slot] = moving
+            came = pull(word, step)
+            take = (came & (1 << step)) != 0
+            words[slot] = jnp.where(take, came - (1 << step), jnp.where(moving != 0, 0, word))
+            comps[slot] = [jnp.where(take, pull(c, step), c) for c in comps[slot]]
+    half = lanes // 2
+    left_half = lax.broadcasted_iota(jnp.int32, (room, lanes), 1) < half
+    for slot in range(slots):
+        columns = comps[slot] + [(words[slot] // receptors).astype(jnp.float32)]
+        for at, column in enumerate(columns):
+            request_ref[slot, at] = jnp.where(
+                left_half, column[:room], pltpu.roll(column[room:], half, 1)
+            )
+
     pl.semaphore_wait(barrier, greeted)
 
     def ask(shift):
         return pltpu.make_async_remote_copy(
-            src_ref=request_ref,
+            src_ref=request_ref.at[shift + REACH],
             dst_ref=asked.at[shift + REACH],
             send_sem=ask_send.at[shift + REACH],
             recv_sem=ask_recv.at[shift + REACH],
@@ -246,6 +343,15 @@
     def weights(layer):
         return plane_ref[...] * float(quad[layer])
 
+    loads[4].wait()
+    loads[5].wait()
+    wall_rows = []
+    for side in range(2):
+        wall_row = jnp.zeros((1, elems), jnp.float32)
+        for x in range(EX):
+            bit = wall_ref[side : side + 1, x : x + 1].astype(jnp.float32)
+            wall_row = jnp.where(x_index[0:1] == x, bit, wall_row)
+        wall_rows.append(wall_row)
     g_x, g_y, g_z, g_m = [geometry_ref[d : d + 1, :] for d in range(4)]
 
     diag_plane = jnp.zeros((8, 8, elems), jnp.float32) + g_m
@@ -257,8 +363,8 @@
         image[layer] = plane_sum(
             weights(layer) * (diag_plane + g_z * float(stiff[layer, layer]))
         )
-    wall_low = flag(y_index == 0) * wall_ref[0:1, :]
-    wall_high = flag(y_index == EY - 1) * wall_ref[1:2, :]
+    wall_low = flag(y_index == 0) * wall_rows[0]
+    wall_high = flag(y_index == EY - 1) * wall_rows[1]
     nothing = jnp.zeros((6, 8, elems), jnp.float32)
     wall_plane = plane_sum(jnp.concatenate([wall_low[None], nothing, wall_high[None]], 0))
     faces[0, 0] = image[0]
@@ -268,13 +374,13 @@
     send_faces(0)
     send_faces(1)
 
-    donor_load.wait()
+    loads[3].wait()
     donors = donor_ref[...].reshape(fields * 512, elems)
     coarse = donors.astype(jnp.bfloat16)
     split[:, :elems] = coarse
     split[:, elems:] = (donors - coarse.astype(jnp.float32)).astype(jnp.bfloat16)
 
-    code = lax.broadcasted_iota(jnp.int32, (elems, CHUNK), 0) + slab * elems
+    code = lax.broadcasted_iota(jnp.int32, (elems, CHUNK), 0)
     code = code.astype(jnp.float32)
     basis = lax.broadcasted_iota(jnp.int32, (8, CHUNK), 0)
     norms = [
@@ -297,11 +403,21 @@
         def _():
             ask(shift).wait_recv()
 
-            def part(chunk, carry):
-                block = asked[shift + REACH, :, pl.ds(pl.multiple_of(chunk * CHUNK, CHUNK), CHUNK)]
-                chosen = jnp.where(block[3:4, :] == code, 1.0, 0.0).astype(jnp.bfloat16)
+            group = CHUNK // lanes
+            for chunk in range(room // group):
+                block = [
+                    jnp.concatenate(
+                        [
+                            asked[shift + REACH, c, chunk * group + t : chunk * group + t + 1, :]
+                            for t in range(group)
+                        ],
+                        1,
+                    )
+                    for c in range(4)
+                ]
+                chosen = jnp.where(block[3] == code, 1.0, 0.0).astype(jnp.bfloat16)
                 chosen = jnp.concatenate([chosen, chosen], 0)
-                w_x, w_y, w_z = [lagrange(block[d : d + 1, :]) for d in range(3)]
+                w_x, w_y, w_z = [lagrange(block[d]) for d in range(3)]
                 found = jnp.dot(split[...], chosen, preferred_element_type=jnp.float32)
                 for field in range(fields):
                     cube = found[field * 512 : (field + 1) * 512].reshape(8, 64, CHUNK)
@@ -312,12 +428,13 @@
                     line = total[0] * w_y[0:1, :]
                     for j in range(1, 8):
                         line = line + total[j] * w_y[j : j + 1, :]
-                    answer[shift + REACH, field, pl.ds(chunk, 1), :] = jnp.sum(
-                        line * w_x, axis=0, keepdims=True
-                    )
-                return carry
-
-            lax.fori_loop(0, receptors // CHUNK, part, 0)
+                    value = jnp.sum(line * w_x, axis=0, keepdims=True)
+                    for t in range(group):
+                        row = chunk * group + t
+                        answer[shift + REACH, field, row : row + 1, :] = value[
+                            :, t * lanes : (t + 1) * lanes
+                        ]
+
             reply(shift).start()
 
         return carry
@@ -354,7 +471,6 @@
         free[layer] = open_part
         inverse[layer] = open_part / image[layer]
 
-    interface_sum = jnp.zeros((fields, receptors // CHUNK, CHUNK), jnp.float32)
     for shift in range(-REACH, REACH + 1):
 
         @pl.when(jnp.logical_not(inside(slab + shift)))
@@ -365,20 +481,29 @@
         def _():
             reply(shift).wait_recv()
 
-    for shift in range(-REACH, REACH + 1):
-        interface_sum = interface_sum + answered[shift + REACH]
-    for chunk in range(receptors // CHUNK):
-        interface_ref[:, chunk * CHUNK : (chunk + 1) * CHUNK] = interface_sum[:, chunk, :]
-
-    rows = interface_sum[0]
-    groups = CHUNK // 64
-    rows = jnp.concatenate([rows[:, t * 64 : (t + 1) * 64] for t in range(groups)], 0)
-    count = receptors // CHUNK
-    per_side = count // 2
-    row = lax.broadcasted_iota(jnp.int32, (groups * count, elems), 0)
-    spot = lax.broadcasted_iota(jnp.int32, (groups * count, elems), 1)
-    piece = row % count
-    target = (groups * (piece % per_side) + row // count) * EX + (EX - 1) * (piece // per_side)
+    def gather_field(field):
+        result = jnp.zeros((height, lanes), jnp.float32)
+        for slot in range(slots):
+            packed = answered[slot, field]
+            tile = jnp.concatenate([packed, pltpu.roll(packed, half, 1)], 0)
+            for step in reversed(range(steps)):
+                tile = jnp.where(moves[step, slot] != 0, push(tile, step), tile)
+            result = jnp.where(members[slot], tile, result)
+        return result
+
+    values = [gather_field(field) for field in range(fields)]
+    for row in range(height):
+        interface_ref[:, row * lanes : (row + 1) * lanes] = jnp.concatenate(
+            [value[row : row + 1] for value in values], 0
+        )
+
+    groups = lanes // 64
+    rows = jnp.concatenate([values[0][:, t * 64 : (t + 1) * 64] for t in range(groups)], 0)
+    per_side = height // 2
+    row = lax.broadcasted_iota(jnp.int32, (groups * height, elems), 0)
+    spot = lax.broadcasted_iota(jnp.int32, (groups * height, elems), 1)
+    piece = row % height
+    target = (groups * (piece % per_side) + row // height) * EX + (EX - 1) * (piece // per_side)
     placed = lax.dot_general(
         rows,
         flag(spot == target),
@@ -416,7 +541,7 @@
         total = g_x * along_x + g_y * along_y + g_z * along_z + g_m * tile
         return weights(layer) * total
 
-    forcing_load.wait()
+    loads[6].wait()
     for layer in ORDER:
         loaded = weights(layer) * g_m * forcing_ref[layer] - local_tile(boundary, layer)
         residual_ref[layer] = plane_sum(loaded)
@@ -488,42 +613,59 @@
             reply(shift).wait_send()
 
 
+def flush(*refs):
+    count = (len(refs) - 1) // 2
+    sem = refs[-1]
+    copies = [
+        pltpu.make_async_copy(refs[at], refs[count + at], sem.at[at]) for at in range(count)
+    ]
+    for copy in copies:
+        copy.start()
+    for copy in copies:
+        copy.wait()
+
+
 def body(n, donor_fields, interp_weights, donor_owner, donor_element, geometry, wall_flag, forcing):
-    points, _, _ = gll_tables()
     fields = donor_fields.shape[0]
     elems = geometry.shape[1]
     receptors = donor_element.shape[0]
     slots = 2 * REACH + 1
-    nodes = jnp.asarray(points, jnp.float32)
-    position = jnp.sum(interp_weights * nodes[None, :, None], axis=1)
-    code = (donor_owner[:, 0] * elems + donor_element).astype(jnp.float32)
-    request = jnp.concatenate([position, code[None, :]], 0)
-    walls = jnp.tile(wall_flag.astype(jnp.float32), (1, elems // wall_flag.shape[1]))
-    count = receptors // CHUNK
+    lanes = 128
+    count = receptors // lanes
     cube = (8, 8, 8, elems)
     phases = 4 + ITERS
+    room = count // 2
     vmem = pl.BlockSpec(memory_space=pltpu.VMEM)
-    hbm = pl.BlockSpec(memory_space=pl.ANY)
-    velocity, residual, interface = pl.pallas_call(
+    hbm = pl.BlockSpec(memory_space=pltpu.HBM)
+    shapes = (
+        jax.ShapeDtypeStruct(cube, jnp.float32),
+        jax.ShapeDtypeStruct(cube, jnp.float32),
+        jax.ShapeDtypeStruct((fields, receptors), jnp.float32),
+    )
+    outputs = pl.pallas_call(
         functools.partial(kernel, n),
-        out_shape=(
-            jax.ShapeDtypeStruct(cube, jnp.float32),
-            jax.ShapeDtypeStruct(cube, jnp.float32),
-            jax.ShapeDtypeStruct((fields, receptors), jnp.float32),
-        ),
-        in_specs=[vmem, hbm, vmem, vmem, hbm],
+        out_shape=shapes,
+        in_specs=[hbm] * 7,
         out_specs=(vmem, vmem, vmem),
         scratch_shapes=[
             pltpu.VMEM((fields, 512, elems), jnp.float32),
             pltpu.VMEM(cube, jnp.float32),
+            pltpu.VMEM(interp_weights.shape, jnp.float32),
+            pltpu.VMEM((count, lanes), jnp.int32),
+            pltpu.VMEM((count, lanes), jnp.int32),
+            pltpu.VMEM(geometry.shape, jnp.float32),
+            pltpu.VMEM(wall_flag.shape, jnp.int32),
+            pltpu.VMEM((3, count, lanes), jnp.float32),
+            pltpu.VMEM((slots, 4, room, lanes), jnp.float32),
+            pltpu.VMEM((receptors.bit_length() - 1, slots, count, lanes), jnp.int32),
             pltpu.VMEM(cube, jnp.float32),
             pltpu.VMEM((8, 8, elems), jnp.float32),
             pltpu.VMEM((8, 8, elems), jnp.float32),
-            pltpu.SemaphoreType.DMA((2,)),
+            pltpu.SemaphoreType.DMA((7,)),
             pltpu.VMEM((fields * 512, 2 * elems), jnp.bfloat16),
-            pltpu.VMEM((slots, 4, receptors), jnp.float32),
-            pltpu.VMEM((slots, fields, count, CHUNK), jnp.float32),
-            pltpu.VMEM((slots, fields, count, CHUNK), jnp.float32),
+            pltpu.VMEM((slots, 4, room, lanes), jnp.float32),
+            pltpu.VMEM((slots, fields, room, lanes), jnp.float32),
+            pltpu.VMEM((slots, fields, room, lanes), jnp.float32),
             pltpu.VMEM((phases, 2, 8, 8, elems), jnp.float32),
             pltpu.VMEM((phases, 2, 8, 8, elems), jnp.float32),
             pltpu.VMEM((ITERS, 2, 128), jnp.float32),
@@ -534,15 +676,24 @@
         + [pltpu.SemaphoreType.DMA((phases, 2))] * 2
         + [pltpu.SemaphoreType.DMA((ITERS, n))] * 2,
         compiler_params=pltpu.CompilerParams(
-            collective_id=0, has_side_effects=True, vmem_limit_bytes=48 * 1024 * 1024
+            collective_id=0, has_side_effects=True, vmem_limit_bytes=67043328
         ),
     )(
-        request,
         donor_fields,
+        interp_weights,
+        donor_owner.reshape(count, lanes),
+        donor_element.reshape(count, lanes),
         geometry,
-        walls,
+        wall_flag,
         forcing.reshape(cube),
     )
+    velocity, residual, interface = pl.pallas_call(
+        flush,
+        out_shape=shapes,
+        in_specs=[vmem] * 3,
+        out_specs=(hbm,) * 3,
+        scratch_shapes=[pltpu.SemaphoreType.DMA((3,))],
+    )(*outputs)
     return (velocity.reshape(512, elems), residual.reshape(512, elems), interface)
 
 

time: 66.7 us -> 52.5 us (0.79)
  Pallas kernels: 57.5 us -> 51.7 us
  local copies, waits for them, and re-layouts: 5.07 us -> 0 us
  other arithmetic: 3.17 us -> 0 us
    pallas_call x1 -> x2, Pallas kernels: 57.5 us -> 51.7 us  [the longest x1 49.8 us: body(): pl.pallas_call(functools.partial(kernel, n), out_shape=shapes, in_specs=[...]
    unnamed x9 -> x0, local copies, waits for them, and re-layouts: 4.98 us -> none
    convert_element_type x2 -> x0, other arithmetic: 1.38 us -> none  [the longest x1 0.7 us: body(): code = (donor_owner[:, 0] * elems + donor_element).astype(jnp.float32)]
    reduce_sum x1 -> x0, other arithmetic: 1.06 us -> none  [body(): position = jnp.sum(interp_weights * nodes[None, :, None], axis=1)]
    mul x1 -> x0, other arithmetic: 0.7 us -> none  [body(): code = (donor_owner[:, 0] * elems + donor_element).astype(jnp.float32)]
where the time goes in v1:
time: 52.5 us; the launch traced here: 52.3 us
  Pallas kernels  51.7 us (98%)
  between operations  0.64 us (1%)
    pallas_call x1, Pallas kernels, body(): pl.pallas_call(functools.partial(kernel, n), out_shape=shapes, in_specs=[...  49.8 us
    pallas_call x1, Pallas kernels, body(): pl.pallas_call(flush, out_shape=shapes, in_specs=[vmem] * 3, out_specs=(h...  1.86 us

profile of v1, /device:TPU:0, one launch (start us, length us, event | category | flops | bytes accessed | tf_op | source)
XLA Modules:
  0.0 52.3 jit_solution(14739278604048140503)
XLA Ops:
  0.6 49.8 %shard_map.94 = (f32[8,8,8,128]{3,2,1,0:T(8,128)}, f32[8,8,8,128]{3,2,1,0:T(8,128)}, f32[5,2048]{1,0:T(8,128)}) custom-call(f32[5,512,128]{2,1,0:T(8,128)} %donor_hbm.1, f32[3,8,2048]{2,1,0:T(8,128)} %weights_hbm.1, s32[16,128]{1,0:T(8,128)} %bitcast.6, s32[16,128]{1,0:T(8,128)} %bitcast.7, f32[4,128]{1,0:T(4,128)} %geometry_hbm.1, s32[2,8]{1,0:T(2,128)} %wall_hbm.1, ...), custom_call_target="tpu_custom_call" | custom-call | tf_op jit(solution)/shard_map/pallas_call | solution.py:645
  50.5 1.9 %shard_map.95 = (f32[8,8,8,128]{3,2,1,0:T(8,128)}, f32[8,8,8,128]{3,2,1,0:T(8,128)}, f32[5,2048]{1,0:T(8,128)}) custom-call(f32[8,8,8,128]{3,2,1,0:T(8,128)} %get-tuple-element.9.refs_0_, f32[8,8,8,128]{3,2,1,0:T(8,128)} %get-tuple-element.10.refs_1_, f32[5,2048]{1,0:T(8,128)} %get-tuple-element.11.refs_2_), custom_call_target="tpu_custom_call" | custom-call | tf_op jit(solution)/shard_map/pallas_call | solution.py:690

commit v2 on v1

--- a/solution.py
+++ b/solution.py
@@ -14,6 +14,7 @@
 REACH = 2
 CHUNK = 256
 ORDER = (0, 7, 1, 2, 3, 4, 5, 6)
+SHIFTS = (1.5, 0.5)
 MESH = pl.DeviceIdType.MESH
 
 
@@ -46,6 +47,26 @@
     return (abscissae, derivative, quad_weights)
 
 
+def solve(found):
+    matrix = [
+        [found[(min(a, b), max(a, b))] for b in range(ITERS)] for a in range(ITERS)
+    ]
+    right = [found[a] for a in range(ITERS)]
+    for a in range(ITERS):
+        for b in range(a + 1, ITERS):
+            factor = matrix[b][a] / matrix[a][a]
+            for c in range(a + 1, ITERS):
+                matrix[b][c] = matrix[b][c] - factor * matrix[a][c]
+            right[b] = right[b] - factor * right[a]
+    answer = [None] * ITERS
+    for a in reversed(range(ITERS)):
+        total = right[a]
+        for b in range(a + 1, ITERS):
+            total = total - matrix[a][b] * answer[b]
+        answer[a] = total / matrix[a][a]
+    return answer
+
+
 def kernel(
     n,
     donor_hbm,
@@ -55,8 +76,11 @@
     geometry_hbm,
     wall_hbm,
     forcing_hbm,
-    velocity_ref,
-    residual_ref,
+    velocity_hbm,
+    residual_hbm,
+    interface_hbm,
+    velocity,
+    residual,
     interface_ref,
     donor_ref,
     forcing_ref,
@@ -67,7 +91,7 @@
     wall_ref,
     position_ref,
     request_ref,
-    moves,
+    ranks,
     along_y_ref,
     along_x_ref,
     plane_ref,
@@ -80,10 +104,13 @@
     halo,
     dots,
     all_dots,
-    state,
-    image,
-    direction,
-    direction_image,
+    vectors,
+    images,
+    partial,
+    rho,
+    rim,
+    rim_halo,
+    geometry_halo,
     inverse,
     free,
     sharing,
@@ -96,6 +123,11 @@
     face_recv,
     dot_send,
     dot_recv,
+    rim_send,
+    rim_recv,
+    geometry_send,
+    geometry_recv,
+    store_sem,
 ):
     points, derivative, quad = gll_tables()
     stiff = (derivative.T * quad) @ derivative / quad[:, None]
@@ -144,8 +176,9 @@
                 barrier, inc=1, device_id=(other, slab + shift), device_id_type=MESH
             )
 
-    for load in loads[:3]:
-        load.wait()
+    with jax.named_scope('w_loads'):
+        for load in loads[:3]:
+            load.wait()
     depth = lax.broadcasted_iota(jnp.int32, (8, lanes), 0)
     ladder = jnp.zeros((8, lanes), jnp.float32)
     for a in range(8):
@@ -171,6 +204,7 @@
     rank = jnp.dot(block, left, preferred_element_type=jnp.float32)
     rank = rank + jnp.dot(lower, marks, preferred_element_type=jnp.float32)
     rank = rank.astype(jnp.int32)
+    ranks[...] = rank
     row_index = lax.broadcasted_iota(jnp.int32, (height, lanes), 0)
     place = lax.broadcasted_iota(jnp.int32, (height, lanes), 1) * height + row_index
     row_bits = height.bit_length() - 1
@@ -183,14 +217,6 @@
         near = pltpu.roll(tile, height - jump, 0)
         far = pltpu.roll(near, lanes - 1, 1)
         return jnp.where(row_index < height - jump, near, far)
-
-    def push(tile, step):
-        if step >= row_bits:
-            return pltpu.roll(tile, 1 << (step - row_bits), 1)
-        jump = 1 << step
-        near = pltpu.roll(tile, jump, 0)
-        far = pltpu.roll(near, 1, 1)
-        return jnp.where(row_index >= jump, near, far)
 
     words = []
     comps = []
@@ -203,7 +229,6 @@
         for slot in range(slots):
             word = words[slot]
             moving = word & (1 << step)
-            moves[step, slot] = moving
             came = pull(word, step)
             take = (came & (1 << step)) != 0
             words[slot] = jnp.where(take, came - (1 << step), jnp.where(moving != 0, 0, word))
@@ -211,13 +236,14 @@
     half = lanes // 2
     left_half = lax.broadcasted_iota(jnp.int32, (room, lanes), 1) < half
     for slot in range(slots):
-        columns = comps[slot] + [(words[slot] // receptors).astype(jnp.float32)]
+        columns = comps[slot] + [(words[slot] >> steps).astype(jnp.float32)]
         for at, column in enumerate(columns):
             request_ref[slot, at] = jnp.where(
                 left_half, column[:room], pltpu.roll(column[room:], half, 1)
             )
 
-    pl.semaphore_wait(barrier, greeted)
+    with jax.named_scope('w_barrier'):
+        pl.semaphore_wait(barrier, greeted)
 
     def ask(shift):
         return pltpu.make_async_remote_copy(
@@ -276,15 +302,48 @@
         def _():
             face_copy(phase, False).wait_send()
 
-    def dot_copy(turn, step):
+    def dot_copy(step):
         return pltpu.make_async_remote_copy(
-            src_ref=dots.at[turn],
-            dst_ref=all_dots.at[turn, slab],
-            send_sem=dot_send.at[turn, step],
-            recv_sem=dot_recv.at[turn, step],
+            src_ref=dots,
+            dst_ref=all_dots.at[slab],
+            send_sem=dot_send.at[step],
+            recv_sem=dot_recv.at[step],
             device_id=(mesh_id, lax.rem(slab + step, n)),
             device_id_type=MESH,
         )
+
+    rim_jumps = (1, -1, 2, -2)
+    rim_sends = [inside(slab + jump) for jump in rim_jumps]
+    rim_comes = [inside(slab - jump) for jump in rim_jumps]
+    near = (slab > 0, slab < n - 1)
+
+    def rim_copy(at):
+        return pltpu.make_async_remote_copy(
+            src_ref=rim.at[1 - at % 2],
+            dst_ref=rim_halo.at[at],
+            send_sem=rim_send.at[at],
+            recv_sem=rim_recv.at[at],
+            device_id=(mesh_id, lax.rem(slab + rim_jumps[at] + n, n)),
+            device_id_type=MESH,
+        )
+
+    def geometry_copy(up):
+        side = 0 if up else 1
+        return pltpu.make_async_remote_copy(
+            src_ref=geometry_ref,
+            dst_ref=geometry_halo.at[side],
+            send_sem=geometry_send.at[side],
+            recv_sem=geometry_recv.at[side],
+            device_id=(mesh_id, lax.rem(slab + (1 if up else n - 1), n)),
+            device_id_type=MESH,
+        )
+
+    stores = [
+        pltpu.make_async_copy(source, target, store_sem.at[at])
+        for at, (source, target) in enumerate(
+            ((interface_ref, interface_hbm), (velocity, velocity_hbm), (rho, residual_hbm))
+        )
+    ]
 
     for distance in range(REACH + 1):
         for shift in sorted({distance, -distance}):
@@ -295,6 +354,18 @@
 
     phases = halo.shape[0]
     blank = jnp.zeros(halo.shape[2:], jnp.float32)
+
+    for at in range(4):
+
+        @pl.when(jnp.logical_not(rim_comes[at]))
+        def _():
+            rim_halo[at] = jnp.zeros(rim_halo.shape[1:], jnp.float32)
+
+    for side in range(2):
+
+        @pl.when(jnp.logical_not(near[side]))
+        def _():
+            geometry_halo[side] = jnp.zeros(geometry_halo.shape[1:], jnp.float32)
 
     @pl.when(slab == 0)
     def _():
@@ -345,6 +416,15 @@
 
     loads[4].wait()
     loads[5].wait()
+
+    @pl.when(near[1])
+    def _():
+        geometry_copy(True).start()
+
+    @pl.when(near[0])
+    def _():
+        geometry_copy(False).start()
+
     wall_rows = []
     for side in range(2):
         wall_row = jnp.zeros((1, elems), jnp.float32)
@@ -360,21 +440,22 @@
         [(g_y * float(stiff[j, j]) + jnp.zeros((8, elems), jnp.float32))[None] for j in range(8)], 0
     )
     for layer in ORDER:
-        image[layer] = plane_sum(
+        images[0, layer] = plane_sum(
             weights(layer) * (diag_plane + g_z * float(stiff[layer, layer]))
         )
     wall_low = flag(y_index == 0) * wall_rows[0]
     wall_high = flag(y_index == EY - 1) * wall_rows[1]
     nothing = jnp.zeros((6, 8, elems), jnp.float32)
     wall_plane = plane_sum(jnp.concatenate([wall_low[None], nothing, wall_high[None]], 0))
-    faces[0, 0] = image[0]
-    faces[0, 1] = image[7]
+    faces[0, 0] = images[0, 0]
+    faces[0, 1] = images[0, 7]
     faces[1, 0] = wall_plane
     faces[1, 1] = wall_plane
     send_faces(0)
     send_faces(1)
 
-    loads[3].wait()
+    with jax.named_scope('w_donor'):
+        loads[3].wait()
     donors = donor_ref[...].reshape(fields * 512, elems)
     coarse = donors.astype(jnp.bfloat16)
     split[:, :elems] = coarse
@@ -401,7 +482,8 @@
 
         @pl.when(inside(slab - shift))
         def _():
-            ask(shift).wait_recv()
+            with jax.named_scope('w_ask'):
+                ask(shift).wait_recv()
 
             group = CHUNK // lanes
             for chunk in range(room // group):
@@ -435,7 +517,8 @@
                             :, t * lanes : (t + 1) * lanes
                         ]
 
-            reply(shift).start()
+            with jax.named_scope('reply'):
+                reply(shift).start()
 
         return carry
 
@@ -453,10 +536,11 @@
         0,
     )
     mark = flag((node == 0) & (x_index == 0)) + flag((node == 7) & (x_index == EX - 1))
-    wait_faces(0)
-    wait_faces(1)
-    image[0] = image[0] + halo[0, 0]
-    image[7] = image[7] + halo[0, 1]
+    with jax.named_scope('w_f01'):
+        wait_faces(0)
+        wait_faces(1)
+    images[0, 0] = images[0, 0] + halo[0, 0]
+    images[0, 7] = images[0, 7] + halo[0, 1]
     for layer in range(8):
         count = plane_count
         walls = wall_plane
@@ -469,7 +553,7 @@
         open_part = 1.0 - jnp.minimum(mark * count + walls, 1.0)
         sharing[layer] = 1.0 / count
         free[layer] = open_part
-        inverse[layer] = open_part / image[layer]
+        inverse[layer] = open_part / images[0, layer]
 
     for shift in range(-REACH, REACH + 1):
 
@@ -479,24 +563,48 @@
 
         @pl.when(inside(slab + shift))
         def _():
-            reply(shift).wait_recv()
+            with jax.named_scope('w_reply'):
+                reply(shift).wait_recv()
+
+    room_index = lax.broadcasted_iota(jnp.int32, (room, lanes), 0)
+    plans = []
+    for slot in range(slots):
+        table = ranks[slot * height : (slot + 1) * height, :]
+        base = jnp.broadcast_to(table[0:1], (room, lanes))
+        first = jnp.minimum(base >> row_bits, half - 1)
+        second = jnp.minimum(first + 1, half - 1)
+        offset = base & (height - 1)
+        spots = table & (height - 1)
+        plans.append((first, second, offset, spots))
+
+    def along_lanes(tile, index):
+        return jnp.take_along_axis(tile, index, axis=1, mode="promise_in_bounds")
+
+    def along_rows(tile, index):
+        return jnp.take_along_axis(tile, index, axis=0, mode="promise_in_bounds")
 
     def gather_field(field):
-        result = jnp.zeros((height, lanes), jnp.float32)
+        result = [jnp.zeros((room, lanes), jnp.float32)] * 2
         for slot in range(slots):
             packed = answered[slot, field]
-            tile = jnp.concatenate([packed, pltpu.roll(packed, half, 1)], 0)
-            for step in reversed(range(steps)):
-                tile = jnp.where(moves[step, slot] != 0, push(tile, step), tile)
-            result = jnp.where(members[slot], tile, result)
-        return result
-
-    values = [gather_field(field) for field in range(fields)]
-    for row in range(height):
-        interface_ref[:, row * lanes : (row + 1) * lanes] = jnp.concatenate(
-            [value[row : row + 1] for value in values], 0
-        )
-
+            first, second, offset, spots = plans[slot]
+            windows = [
+                jnp.where(
+                    room_index + part * room >= offset,
+                    along_lanes(packed, first + part * half),
+                    along_lanes(packed, second + part * half),
+                )
+                for part in range(2)
+            ]
+            for part in range(2):
+                spot = spots[part * room : (part + 1) * room]
+                member = members[slot][part * room : (part + 1) * room]
+                low, high = [along_rows(window, spot & (room - 1)) for window in windows]
+                tile = jnp.where(spot < room, low, high)
+                result[part] = jnp.where(member, tile, result[part])
+        return jnp.concatenate(result, 0)
+
+    values = [gather_field(0)]
     groups = lanes // 64
     rows = jnp.concatenate([values[0][:, t * 64 : (t + 1) * 64] for t in range(groups)], 0)
     per_side = height // 2
@@ -511,96 +619,221 @@
         precision=lax.Precision.HIGHEST,
         preferred_element_type=jnp.float32,
     ).reshape(8, 8, elems)
-    for layer in ORDER:
-        spread = jnp.concatenate(
-            [(jnp.broadcast_to(placed[layer, j : j + 1, :], (8, elems)) * mark)[None] for j in range(8)],
-            0,
-        )
-        boundary[layer] = plane_sum(spread)
-        if layer == 7:
-            faces[2, 0] = boundary[0]
-            faces[2, 1] = boundary[7]
-            send_faces(2)
-    wait_faces(2)
-    boundary[0] = boundary[0] + halo[2, 0]
-    boundary[7] = boundary[7] + halo[2, 1]
-    for layer in range(8):
-        boundary[layer] = boundary[layer] * sharing[layer]
-
-    def local_tile(source, layer):
-        tile = source[layer]
-        along_z = source[0] * float(stiff[layer, 0])
-        for k in range(1, 8):
-            along_z = along_z + source[k] * float(stiff[layer, k])
+    rim[0] = placed[0]
+    rim[1] = placed[7]
+    for at in range(4):
+
+        @pl.when(rim_sends[at])
+        def _():
+            rim_copy(at).start()
+
+    def spread_out(column):
+        return plane_sum(
+            jnp.concatenate(
+                [
+                    (jnp.broadcast_to(column[j : j + 1, :], (8, elems)) * mark)[None]
+                    for j in range(8)
+                ],
+                0,
+            )
+        )
+
+    def in_plane(tile, along):
         along_y = along_y_ref[0] * tile[0:1]
         for j in range(1, 8):
             along_y = along_y + along_y_ref[j] * tile[j : j + 1]
         along_x = along_x_ref[0] * tile
         for step in range(1, 8):
             along_x = along_x + along_x_ref[step] * pltpu.roll(tile, step, 1)
-        total = g_x * along_x + g_y * along_y + g_z * along_z + g_m * tile
-        return weights(layer) * total
-
+        return along[0] * along_x + along[1] * along_y
+
+    def inner_z(read, layer):
+        total = read(1) * float(stiff[layer, 1])
+        for k in range(2, 7):
+            total = total + read(k) * float(stiff[layer, k])
+        return total
+
+    def outer_z(low, high, layer):
+        return low * float(stiff[layer, 0]) + high * float(stiff[layer, 7])
+
+    here = (g_x, g_y, g_z, g_m)
+    edge = weights(0)
+
+    for layer in ORDER:
+        boundary[layer] = spread_out(placed[layer]) * sharing[layer]
     loads[6].wait()
     for layer in ORDER:
-        loaded = weights(layer) * g_m * forcing_ref[layer] - local_tile(boundary, layer)
-        residual_ref[layer] = plane_sum(loaded)
+        along_z = inner_z(lambda k: boundary[k], layer)
+        along_z = along_z + outer_z(boundary[0], boundary[7], layer)
+        tile = boundary[layer]
+        total = in_plane(tile, here) + g_z * along_z + g_m * (tile - forcing_ref[layer])
+        total = weights(layer) * total
+        if layer in (0, 7):
+            total = plane_sum(total)
+        residual[layer] = total
         if layer == 7:
-            faces[3, 0] = residual_ref[0]
-            faces[3, 1] = residual_ref[7]
-            send_faces(3)
-    wait_faces(3)
-    residual_ref[0] = residual_ref[0] + halo[3, 0]
-    residual_ref[7] = residual_ref[7] + halo[3, 1]
+            faces[2, 0] = residual[0]
+            faces[2, 1] = residual[7]
+            send_faces(2)
+
+    beyond = []
+    for side in range(2):
+
+        @pl.when(near[side])
+        def _():
+            geometry_copy(side == 0).wait_recv()
+
+        along = [geometry_halo[side, d : d + 1, :] for d in range(4)]
+        own = boundary[0 if side == 0 else 7]
+        term = in_plane(own, along)
+        term = term + (along[2] * float(stiff[0, 0]) + along[3]) * own
+        beyond.append((term, along[2] * float(stiff[0, 7])))
+    values = values + [gather_field(field) for field in range(1, fields)]
+    for row in range(height):
+        interface_ref[:, row * lanes : (row + 1) * lanes] = jnp.concatenate(
+            [value[row : row + 1] for value in values], 0
+        )
+    stores[0].start()
+
+    with jax.named_scope('w_rim'):
+        for at in range(4):
+
+            @pl.when(rim_comes[at])
+            def _():
+                rim_copy(at).wait_recv()
+
+    low = spread_out(rim_halo[0]) * sharing[0]
+    high = spread_out(rim_halo[1]) * sharing[7]
+    boundary[0] = boundary[0] + low
+    boundary[7] = boundary[7] + high
+    for layer in range(1, 7):
+        more = weights(layer) * (g_z * outer_z(low, high, layer))
+        residual[layer] = -free[layer] * plane_sum(residual[layer] + more)
+        rho[layer] = residual[layer]
+        vectors[0, layer] = inverse[layer] * residual[layer]
+    half_share = 0.5 / plane_count
+    ends = []
+    for side, (own, layer) in enumerate(((low, 0), (high, 7))):
+        more = in_plane(own, here) + g_m * own + g_z * outer_z(low, high, layer)
+        term, across_z = beyond[side]
+        more = more + term + across_z * (spread_out(rim_halo[2 + side]) * half_share)
+        ends.append(residual[layer] + plane_sum(edge * more))
+
+    def prepare(turn):
+        def read(k):
+            return vectors[turn, k]
+
+        for layer in range(1, 7):
+            tile = vectors[turn, layer]
+            partial[layer] = (
+                in_plane(tile, here) + g_m * tile + g_z * inner_z(read, layer)
+            )
+        for layer in (0, 7):
+            partial[layer] = g_z * inner_z(read, layer)
+
+    prepare(0)
+    with jax.named_scope('w_f2'):
+        wait_faces(2)
+    for side, layer in ((0, 0), (1, 7)):
+        residual[layer] = -free[layer] * (ends[side] + halo[2, side])
+        rho[layer] = residual[layer]
+        vectors[0, layer] = inverse[layer] * residual[layer]
+
+    sums = {}
+
+    def gather_sum(key, value):
+        value = jnp.sum(value, axis=0)
+        sums[key] = value if key not in sums else sums[key] + value
+
+    for turn in range(ITERS):
+        phase = 3 + turn
+        low = vectors[turn, 0]
+        high = vectors[turn, 7]
+        outer = {}
+        for layer in (0, 7):
+            tile = vectors[turn, layer]
+            total = in_plane(tile, here) + g_m * tile + g_z * outer_z(low, high, layer)
+            outer[layer] = edge * (total + partial[layer])
+            images[turn, layer] = plane_sum(outer[layer])
+        faces[phase, 0] = images[turn, 0]
+        faces[phase, 1] = images[turn, 7]
+        send_faces(phase)
+        last = turn == ITERS - 1
+        for layer in range(8):
+            if layer in outer:
+                tile = outer[layer]
+            else:
+                tile = partial[layer] + g_z * outer_z(low, high, layer)
+                tile = weights(layer) * tile
+            for other_turn in range(turn + 1):
+                gather_sum((other_turn, turn), tile * vectors[other_turn, layer])
+            gather_sum(
+                turn, vectors[turn, layer] * residual[layer] * sharing[layer]
+            )
+            if layer not in outer:
+                images[turn, layer] = tile if last else free[layer] * plane_sum(tile)
+        if last:
+            break
+        for layer in range(1, 7):
+            rho[layer] = images[turn, layer] - SHIFTS[turn] * rho[layer]
+            vectors[turn + 1, layer] = inverse[layer] * rho[layer]
+        prepare(turn + 1)
+        with jax.named_scope('w_fc'):
+            wait_faces(phase)
+        for side, layer in ((0, 0), (1, 7)):
+            images[turn, layer] = free[layer] * (images[turn, layer] + halo[phase, side])
+            rho[layer] = images[turn, layer] - SHIFTS[turn] * rho[layer]
+            vectors[turn + 1, layer] = inverse[layer] * rho[layer]
+
+    keys = list(range(ITERS)) + [(a, b) for b in range(ITERS) for a in range(b + 1)]
+    spot = lax.broadcasted_iota(jnp.int32, (1, 128), 1)
+    packed = jnp.zeros((1, 128), jnp.float32)
+    for at, key in enumerate(keys):
+        value = jnp.sum(jnp.sum(sums[key], axis=0, keepdims=True), axis=1, keepdims=True)
+        packed = jnp.where(spot == at, value, packed)
+    dots[...] = packed
+    for step in range(1, n):
+        dot_copy(step).start()
+    all_dots[slab] = dots[...]
+    for layer in range(1, 7):
+        images[ITERS - 1, layer] = free[layer] * plane_sum(images[ITERS - 1, layer])
+    with jax.named_scope('w_fc'):
+        wait_faces(3 + ITERS - 1)
+    for side, layer in ((0, 0), (1, 7)):
+        images[ITERS - 1, layer] = free[layer] * (
+            images[ITERS - 1, layer] + halo[3 + ITERS - 1, side]
+        )
+    with jax.named_scope('w_dots'):
+        for step in range(1, n):
+            dot_copy(step).wait_recv()
+    total = jnp.sum(all_dots[...], axis=0)
+    found = {key: total[:, at : at + 1] for at, key in enumerate(keys)}
+    steps_taken = solve(found)
     for layer in range(8):
-        residual_ref[layer] = residual_ref[layer] * free[layer]
-        velocity_ref[layer] = boundary[layer]
-        direction[layer] = jnp.zeros((8, 8, elems), jnp.float32)
-        direction_image[layer] = jnp.zeros((8, 8, elems), jnp.float32)
-
-    def iterate(turn, carry):
-        norm, length = carry
-        phase = turn + 4
-        norm_part = jnp.zeros((8, 8, elems), jnp.float32)
-        for layer in range(8):
-            state[layer] = inverse[layer] * residual_ref[layer]
-            norm_part = norm_part + state[layer] * residual_ref[layer] * sharing[layer]
-        curve_part = jnp.zeros((8, 8, elems), jnp.float32)
-        for layer in ORDER:
-            tile = local_tile(state, layer)
-            curve_part = curve_part + tile * state[layer]
-            image[layer] = plane_sum(tile)
-            if layer == 7:
-                faces[phase, 0] = image[0]
-                faces[phase, 1] = image[7]
-                send_faces(phase)
-        dots[turn, 0:1, :] = jnp.sum(jnp.sum(norm_part, axis=0), axis=0, keepdims=True)
-        dots[turn, 1:2, :] = jnp.sum(jnp.sum(curve_part, axis=0), axis=0, keepdims=True)
-        for step in range(1, n):
-            dot_copy(turn, step).start()
-        all_dots[turn, slab] = dots[turn]
-        wait_faces(phase)
-        image[0] = image[0] + halo[phase, 0]
-        image[7] = image[7] + halo[phase, 1]
-        for step in range(1, n):
-            dot_copy(turn, step).wait_recv()
-        sums = jnp.sum(jnp.sum(all_dots[turn], axis=0), axis=1, keepdims=True)
-        norm_next, curvature = sums[0:1, :], sums[1:2, :]
-        ratio = jnp.where(turn == 0, 0.0, norm_next / norm)
-        length = norm_next / (curvature - ratio * norm_next / length)
-        for layer in range(8):
-            toward = state[layer] + ratio * direction[layer]
-            toward_image = free[layer] * image[layer] + ratio * direction_image[layer]
-            direction[layer] = toward
-            direction_image[layer] = toward_image
-            velocity_ref[layer] = velocity_ref[layer] + length * toward
-            residual_ref[layer] = residual_ref[layer] - length * toward_image
-        for step in range(1, n):
-            dot_copy(turn, step).wait_send()
-        return norm_next, length
-
-    one = jnp.ones((1, 1), jnp.float32)
-    lax.fori_loop(0, ITERS, iterate, (one, one))
+        moved = boundary[layer]
+        for turn in range(ITERS):
+            moved = moved + steps_taken[turn] * vectors[turn, layer]
+        velocity[layer] = moved
+    stores[1].start()
+    for layer in range(8):
+        left_over = residual[layer]
+        for turn in range(ITERS):
+            left_over = left_over - steps_taken[turn] * images[turn, layer]
+        rho[layer] = left_over
+    stores[2].start()
+    for step in range(1, n):
+        dot_copy(step).wait_send()
+    for side in range(2):
+
+        @pl.when(near[1 - side])
+        def _():
+            geometry_copy(side == 0).wait_send()
+
+    for at in range(4):
+
+        @pl.when(rim_sends[at])
+        def _():
+            rim_copy(at).wait_send()
 
     for shift in range(-REACH, REACH + 1):
 
@@ -611,6 +844,9 @@
         @pl.when(inside(slab - shift))
         def _():
             reply(shift).wait_send()
+
+    for store in stores:
+        store.wait()
 
 
 def flush(*refs):
@@ -633,7 +869,7 @@
     lanes = 128
     count = receptors // lanes
     cube = (8, 8, 8, elems)
-    phases = 4 + ITERS
+    phases = 3 + ITERS
     room = count // 2
     vmem = pl.BlockSpec(memory_space=pltpu.VMEM)
     hbm = pl.BlockSpec(memory_space=pltpu.HBM)
@@ -646,8 +882,11 @@
         functools.partial(kernel, n),
         out_shape=shapes,
         in_specs=[hbm] * 7,
-        out_specs=(vmem, vmem, vmem),
+        out_specs=(hbm, hbm, hbm),
         scratch_shapes=[
+            pltpu.VMEM(cube, jnp.float32),
+            pltpu.VMEM(cube, jnp.float32),
+            pltpu.VMEM((fields, receptors), jnp.float32),
             pltpu.VMEM((fields, 512, elems), jnp.float32),
             pltpu.VMEM(cube, jnp.float32),
             pltpu.VMEM(interp_weights.shape, jnp.float32),
@@ -657,7 +896,7 @@
             pltpu.VMEM(wall_flag.shape, jnp.int32),
             pltpu.VMEM((3, count, lanes), jnp.float32),
             pltpu.VMEM((slots, 4, room, lanes), jnp.float32),
-            pltpu.VMEM((receptors.bit_length() - 1, slots, count, lanes), jnp.int32),
+            pltpu.VMEM((slots * count, lanes), jnp.int32),
             pltpu.VMEM(cube, jnp.float32),
             pltpu.VMEM((8, 8, elems), jnp.float32),
             pltpu.VMEM((8, 8, elems), jnp.float32),
@@ -668,13 +907,23 @@
             pltpu.VMEM((slots, fields, room, lanes), jnp.float32),
             pltpu.VMEM((phases, 2, 8, 8, elems), jnp.float32),
             pltpu.VMEM((phases, 2, 8, 8, elems), jnp.float32),
-            pltpu.VMEM((ITERS, 2, 128), jnp.float32),
-            pltpu.VMEM((ITERS, n, 2, 128), jnp.float32),
+            pltpu.VMEM((1, 128), jnp.float32),
+            pltpu.VMEM((n, 1, 128), jnp.float32),
+            pltpu.VMEM((ITERS,) + cube, jnp.float32),
+            pltpu.VMEM((ITERS,) + cube, jnp.float32),
+            pltpu.VMEM(cube, jnp.float32),
+            pltpu.VMEM(cube, jnp.float32),
+            pltpu.VMEM((2, 8, elems), jnp.float32),
+            pltpu.VMEM((4, 8, elems), jnp.float32),
+            pltpu.VMEM((2,) + geometry.shape, jnp.float32),
         ]
-        + [pltpu.VMEM(cube, jnp.float32)] * 8
+        + [pltpu.VMEM(cube, jnp.float32)] * 4
         + [pltpu.SemaphoreType.DMA((slots,))] * 4
         + [pltpu.SemaphoreType.DMA((phases, 2))] * 2
-        + [pltpu.SemaphoreType.DMA((ITERS, n))] * 2,
+        + [pltpu.SemaphoreType.DMA((n,))] * 2
+        + [pltpu.SemaphoreType.DMA((4,))] * 2
+        + [pltpu.SemaphoreType.DMA((2,))] * 2
+        + [pltpu.SemaphoreType.DMA((3,))],
         compiler_params=pltpu.CompilerParams(
             collective_id=0, has_side_effects=True, vmem_limit_bytes=67043328
         ),

time: 52.5 us -> 41.2 us (0.78)
  Pallas kernels: 51.7 us -> 40.4 us
    pallas_call x1, Pallas kernels: 49.8 us -> 38.6 us  [body(): pl.pallas_call(functools.partial(kernel, n), out_shape=shapes, in_specs=[...]
where the time goes in v2:
time: 41.2 us; the launch traced here: 41.1 us
  Pallas kernels  40.4 us (98%)
  between operations  0.64 us (2%)
    pallas_call x1, Pallas kernels, body(): pl.pallas_call(functools.partial(kernel, n), out_shape=shapes, in_specs=[...  38.6 us
    pallas_call x1, Pallas kernels, body(): pl.pallas_call(flush, out_shape=shapes, in_specs=[vmem] * 3, out_specs=(h...  1.86 us

profile of v2, /device:TPU:0, one launch (start us, length us, event | category | flops | bytes accessed | tf_op | source)
XLA Modules:
  0.0 41.1 jit_solution(8964831072820529640)
XLA Ops:
  0.6 38.6 %shard_map.94 = (f32[8,8,8,128]{3,2,1,0:T(8,128)}, f32[8,8,8,128]{3,2,1,0:T(8,128)}, f32[5,2048]{1,0:T(8,128)}) custom-call(f32[5,512,128]{2,1,0:T(8,128)} %donor_hbm.1, f32[3,8,2048]{2,1,0:T(8,128)} %weights_hbm.1, s32[16,128]{1,0:T(8,128)} %bitcast.6, s32[16,128]{1,0:T(8,128)} %bitcast.7, f32[4,128]{1,0:T(4,128)} %geometry_hbm.1, s32[2,8]{1,0:T(2,128)} %wall_hbm.1, ...), custom_call_target="tpu_custom_call" | custom-call | tf_op jit(solution)/shard_map/pallas_call | solution.py:881
  39.2 1.9 %shard_map.95 = (f32[8,8,8,128]{3,2,1,0:T(8,128)}, f32[8,8,8,128]{3,2,1,0:T(8,128)}, f32[5,2048]{1,0:T(8,128)}) custom-call(f32[8,8,8,128]{3,2,1,0:T(8,128)} %get-tuple-element.9.refs_0_, f32[8,8,8,128]{3,2,1,0:T(8,128)} %get-tuple-element.10.refs_1_, f32[5,2048]{1,0:T(8,128)} %get-tuple-element.11.refs_2_), custom_call_target="tpu_custom_call" | custom-call | tf_op jit(solution)/shard_map/pallas_call | solution.py:939

commit v3 on v2

--- a/solution.py
+++ b/solution.py
@@ -15,6 +15,7 @@
 CHUNK = 256
 ORDER = (0, 7, 1, 2, 3, 4, 5, 6)
 SHIFTS = (1.5, 0.5)
+WINDOWS = (1, 1)
 MESH = pl.DeviceIdType.MESH
 
 
@@ -52,9 +53,11 @@
         [found[(min(a, b), max(a, b))] for b in range(ITERS)] for a in range(ITERS)
     ]
     right = [found[a] for a in range(ITERS)]
+    pivots = []
     for a in range(ITERS):
+        pivots.append(1.0 / matrix[a][a])
         for b in range(a + 1, ITERS):
-            factor = matrix[b][a] / matrix[a][a]
+            factor = matrix[b][a] * pivots[a]
             for c in range(a + 1, ITERS):
                 matrix[b][c] = matrix[b][c] - factor * matrix[a][c]
             right[b] = right[b] - factor * right[a]
@@ -63,7 +66,7 @@
         total = right[a]
         for b in range(a + 1, ITERS):
             total = total - matrix[a][b] * answer[b]
-        answer[a] = total / matrix[a][a]
+        answer[a] = total * pivots[a]
     return answer
 
 
@@ -111,6 +114,7 @@
     rim,
     rim_halo,
     geometry_halo,
+    packet,
     inverse,
     free,
     sharing,
@@ -255,12 +259,13 @@
             device_id_type=MESH,
         )
 
-    def reply(shift):
+    def reply(shift, part):
+        span = pl.ds(0, 1) if part == 0 else pl.ds(1, fields - 1)
         return pltpu.make_async_remote_copy(
-            src_ref=answer.at[shift + REACH],
-            dst_ref=answered.at[shift + REACH],
-            send_sem=reply_send.at[shift + REACH],
-            recv_sem=reply_recv.at[shift + REACH],
+            src_ref=answer.at[shift + REACH, span],
+            dst_ref=answered.at[shift + REACH, span],
+            send_sem=reply_send.at[part, shift + REACH],
+            recv_sem=reply_recv.at[part, shift + REACH],
             device_id=(other, lax.rem(slab - shift + n, n)),
             device_id_type=MESH,
         )
@@ -330,7 +335,7 @@
     def geometry_copy(up):
         side = 0 if up else 1
         return pltpu.make_async_remote_copy(
-            src_ref=geometry_ref,
+            src_ref=packet,
             dst_ref=geometry_halo.at[side],
             send_sem=geometry_send.at[side],
             recv_sem=geometry_recv.at[side],
@@ -417,14 +422,6 @@
     loads[4].wait()
     loads[5].wait()
 
-    @pl.when(near[1])
-    def _():
-        geometry_copy(True).start()
-
-    @pl.when(near[0])
-    def _():
-        geometry_copy(False).start()
-
     wall_rows = []
     for side in range(2):
         wall_row = jnp.zeros((1, elems), jnp.float32)
@@ -434,98 +431,34 @@
         wall_rows.append(wall_row)
     g_x, g_y, g_z, g_m = [geometry_ref[d : d + 1, :] for d in range(4)]
 
-    diag_plane = jnp.zeros((8, 8, elems), jnp.float32) + g_m
-    diag_plane = diag_plane + g_x * along_x_ref[0]
-    diag_plane = diag_plane + jnp.concatenate(
-        [(g_y * float(stiff[j, j]) + jnp.zeros((8, elems), jnp.float32))[None] for j in range(8)], 0
+    packet[...] = jnp.concatenate(
+        [geometry_ref[...]] + wall_rows + [jnp.zeros((2, elems), jnp.float32)], 0
     )
-    for layer in ORDER:
-        images[0, layer] = plane_sum(
-            weights(layer) * (diag_plane + g_z * float(stiff[layer, layer]))
-        )
-    wall_low = flag(y_index == 0) * wall_rows[0]
-    wall_high = flag(y_index == EY - 1) * wall_rows[1]
+
+    @pl.when(near[1])
+    def _():
+        geometry_copy(True).start()
+
+    @pl.when(near[0])
+    def _():
+        geometry_copy(False).start()
+
+    diag_y = [jnp.full((8, elems), float(stiff[j, j]), jnp.float32)[None] for j in range(8)]
+    diag_y = jnp.concatenate(diag_y, 0)
+
+    def diagonal(along, layer):
+        total = along[0] * along_x_ref[0] + along[1] * diag_y
+        total = total + (along[2] * float(stiff[layer, layer]) + along[3])
+        return plane_sum(weights(layer) * total)
+
     nothing = jnp.zeros((6, 8, elems), jnp.float32)
-    wall_plane = plane_sum(jnp.concatenate([wall_low[None], nothing, wall_high[None]], 0))
-    faces[0, 0] = images[0, 0]
-    faces[0, 1] = images[0, 7]
-    faces[1, 0] = wall_plane
-    faces[1, 1] = wall_plane
-    send_faces(0)
-    send_faces(1)
-
-    with jax.named_scope('w_donor'):
-        loads[3].wait()
-    donors = donor_ref[...].reshape(fields * 512, elems)
-    coarse = donors.astype(jnp.bfloat16)
-    split[:, :elems] = coarse
-    split[:, elems:] = (donors - coarse.astype(jnp.float32)).astype(jnp.bfloat16)
-
-    code = lax.broadcasted_iota(jnp.int32, (elems, CHUNK), 0)
-    code = code.astype(jnp.float32)
-    basis = lax.broadcasted_iota(jnp.int32, (8, CHUNK), 0)
-    norms = [
-        float(1.0 / np.prod([points[a] - points[b] for b in range(8) if b != a])) for a in range(8)
-    ]
-    scale = jnp.zeros((8, CHUNK), jnp.float32)
-    for a in range(8):
-        scale = jnp.where(basis == a, norms[a], scale)
-
-    def lagrange(position):
-        value = scale
-        for b in range(8):
-            value = value * jnp.where(basis == b, 1.0, position - float(points[b]))
-        return value
-
-    def serve(turn, carry):
-        shift = ((turn + 1) // 2) * (2 * (turn % 2) - 1)
-
-        @pl.when(inside(slab - shift))
-        def _():
-            with jax.named_scope('w_ask'):
-                ask(shift).wait_recv()
-
-            group = CHUNK // lanes
-            for chunk in range(room // group):
-                block = [
-                    jnp.concatenate(
-                        [
-                            asked[shift + REACH, c, chunk * group + t : chunk * group + t + 1, :]
-                            for t in range(group)
-                        ],
-                        1,
-                    )
-                    for c in range(4)
-                ]
-                chosen = jnp.where(block[3] == code, 1.0, 0.0).astype(jnp.bfloat16)
-                chosen = jnp.concatenate([chosen, chosen], 0)
-                w_x, w_y, w_z = [lagrange(block[d]) for d in range(3)]
-                found = jnp.dot(split[...], chosen, preferred_element_type=jnp.float32)
-                for field in range(fields):
-                    cube = found[field * 512 : (field + 1) * 512].reshape(8, 64, CHUNK)
-                    total = cube[0] * w_z[0:1, :]
-                    for k in range(1, 8):
-                        total = total + cube[k] * w_z[k : k + 1, :]
-                    total = total.reshape(8, 8, CHUNK)
-                    line = total[0] * w_y[0:1, :]
-                    for j in range(1, 8):
-                        line = line + total[j] * w_y[j : j + 1, :]
-                    value = jnp.sum(line * w_x, axis=0, keepdims=True)
-                    for t in range(group):
-                        row = chunk * group + t
-                        answer[shift + REACH, field, row : row + 1, :] = value[
-                            :, t * lanes : (t + 1) * lanes
-                        ]
-
-            with jax.named_scope('reply'):
-                reply(shift).start()
-
-        return carry
-
-    lax.fori_loop(0, slots, serve, 0)
-
-    z_low = jnp.where(slab > 0, 2.0, 1.0)
-    z_high = jnp.where(slab < n - 1, 2.0, 1.0)
+
+    def wall_marks(rows):
+        low_wall = flag(y_index == 0) * rows[0]
+        high_wall = flag(y_index == EY - 1) * rows[1]
+        return plane_sum(jnp.concatenate([low_wall[None], nothing, high_wall[None]], 0))
+
+    wall_plane = wall_marks(wall_rows)
     x_count = 1.0 + x_low + x_high
     y_count_low = 1.0 + y_low
     y_count_high = 1.0 + y_high
@@ -536,35 +469,105 @@
         0,
     )
     mark = flag((node == 0) & (x_index == 0)) + flag((node == 7) & (x_index == EX - 1))
-    with jax.named_scope('w_f01'):
-        wait_faces(0)
-        wait_faces(1)
-    images[0, 0] = images[0, 0] + halo[0, 0]
-    images[0, 7] = images[0, 7] + halo[0, 1]
-    for layer in range(8):
-        count = plane_count
-        walls = wall_plane
-        if layer == 0:
-            count = count * z_low
-            walls = walls + halo[1, 0]
-        if layer == 7:
-            count = count * z_high
-            walls = walls + halo[1, 1]
+
+    def settle(layer, z_count, walls, diag):
+        count = plane_count * z_count
         open_part = 1.0 - jnp.minimum(mark * count + walls, 1.0)
         sharing[layer] = 1.0 / count
         free[layer] = open_part
-        inverse[layer] = open_part / images[0, layer]
-
-    for shift in range(-REACH, REACH + 1):
-
-        @pl.when(jnp.logical_not(inside(slab + shift)))
-        def _():
-            answered[shift + REACH] = jnp.zeros(answered.shape[1:], jnp.float32)
-
-        @pl.when(inside(slab + shift))
-        def _():
-            with jax.named_scope('w_reply'):
-                reply(shift).wait_recv()
+        inverse[layer] = open_part / diag
+
+    for layer in range(1, 7):
+        settle(layer, 1.0, wall_plane, diagonal((g_x, g_y, g_z, g_m), layer))
+    z_counts = (jnp.where(slab > 0, 2.0, 1.0), jnp.where(slab < n - 1, 2.0, 1.0))
+    for side, layer in ((0, 0), (1, 7)):
+        sharing[layer] = 1.0 / (plane_count * z_counts[side])
+
+    with jax.named_scope('w_donor'):
+        loads[3].wait()
+    donors = donor_ref[...].reshape(fields * 512, elems)
+    coarse = donors.astype(jnp.bfloat16)
+    split[:, :elems] = coarse
+    split[:, elems:] = (donors - coarse.astype(jnp.float32)).astype(jnp.bfloat16)
+
+    code = lax.broadcasted_iota(jnp.int32, (elems, CHUNK), 0)
+    code = code.astype(jnp.float32)
+    basis = lax.broadcasted_iota(jnp.int32, (8, CHUNK), 0)
+    norms = [
+        float(1.0 / np.prod([points[a] - points[b] for b in range(8) if b != a])) for a in range(8)
+    ]
+    scale = jnp.zeros((8, CHUNK), jnp.float32)
+    for a in range(8):
+        scale = jnp.where(basis == a, norms[a], scale)
+
+    def lagrange(position):
+        value = scale
+        for b in range(8):
+            value = value * jnp.where(basis == b, 1.0, position - float(points[b]))
+        return value
+
+    def evaluate(shift, first, last):
+        group = CHUNK // lanes
+        for chunk in range(room // group):
+            block = [
+                jnp.concatenate(
+                    [
+                        asked[shift + REACH, c, chunk * group + t : chunk * group + t + 1, :]
+                        for t in range(group)
+                    ],
+                    1,
+                )
+                for c in range(4)
+            ]
+            chosen = jnp.where(block[3] == code, 1.0, 0.0).astype(jnp.bfloat16)
+            chosen = jnp.concatenate([chosen, chosen], 0)
+            w_x, w_y, w_z = [lagrange(block[d]) for d in range(3)]
+            picked = jnp.dot(
+                split[first * 512 : last * 512], chosen, preferred_element_type=jnp.float32
+            )
+            for field in range(first, last):
+                cube = picked[(field - first) * 512 : (field - first + 1) * 512]
+                cube = cube.reshape(8, 64, CHUNK)
+                total = cube[0] * w_z[0:1, :]
+                for k in range(1, 8):
+                    total = total + cube[k] * w_z[k : k + 1, :]
+                total = total.reshape(8, 8, CHUNK)
+                line = total[0] * w_y[0:1, :]
+                for j in range(1, 8):
+                    line = line + total[j] * w_y[j : j + 1, :]
+                value = jnp.sum(line * w_x, axis=0, keepdims=True)
+                for t in range(group):
+                    row = chunk * group + t
+                    answer[shift + REACH, field, row : row + 1, :] = value[
+                        :, t * lanes : (t + 1) * lanes
+                    ]
+
+    def serve(turn, carry):
+        shift = ((turn + 1) // 2) * (2 * (turn % 2) - 1)
+
+        @pl.when(inside(slab - shift))
+        def _():
+            with jax.named_scope('w_ask'):
+                ask(shift).wait_recv()
+            evaluate(shift, 0, 1)
+            with jax.named_scope('reply'):
+                reply(shift, 0).start()
+
+        return carry
+
+    lax.fori_loop(0, slots, serve, 0)
+    turns_left = list(range(slots))
+
+    def serve_rest(many):
+        for _ in range(many):
+            turn = turns_left.pop(0)
+            shift = ((turn + 1) // 2) * (2 * (turn % 2) - 1)
+
+            @pl.when(inside(slab - shift))
+            def _():
+                with jax.named_scope('rest'):
+                    evaluate(shift, 1, fields)
+                reply(shift, 1).start()
 
     room_index = lax.broadcasted_iota(jnp.int32, (room, lanes), 0)
     plans = []
@@ -576,6 +579,18 @@
         offset = base & (height - 1)
         spots = table & (height - 1)
         plans.append((first, second, offset, spots))
+
+    serve_rest(2)
+    for shift in range(-REACH, REACH + 1):
+
+        @pl.when(jnp.logical_not(inside(slab + shift)))
+        def _():
+            answered[shift + REACH] = jnp.zeros(answered.shape[1:], jnp.float32)
+
+        @pl.when(inside(slab + shift))
+        def _():
+            with jax.named_scope('w_reply'):
+                reply(shift, 0).wait_recv()
 
     def along_lanes(tile, index):
         return jnp.take_along_axis(tile, index, axis=1, mode="promise_in_bounds")
@@ -672,9 +687,9 @@
             total = plane_sum(total)
         residual[layer] = total
         if layer == 7:
-            faces[2, 0] = residual[0]
-            faces[2, 1] = residual[7]
-            send_faces(2)
+            faces[0, 0] = residual[0]
+            faces[0, 1] = residual[7]
+            send_faces(0)
 
     beyond = []
     for side in range(2):
@@ -688,12 +703,10 @@
         term = in_plane(own, along)
         term = term + (along[2] * float(stiff[0, 0]) + along[3]) * own
         beyond.append((term, along[2] * float(stiff[0, 7])))
-    values = values + [gather_field(field) for field in range(1, fields)]
-    for row in range(height):
-        interface_ref[:, row * lanes : (row + 1) * lanes] = jnp.concatenate(
-            [value[row : row + 1] for value in values], 0
-        )
-    stores[0].start()
+        walls = wall_plane + wall_marks([geometry_halo[side, 4:5, :], geometry_halo[side, 5:6, :]])
+        layer, facing = (0, 7) if side == 0 else (7, 0)
+        settle(layer, z_counts[side], walls, diagonal(here, layer) + diagonal(along, facing))
+    serve_rest(1)
 
     with jax.named_scope('w_rim'):
         for at in range(4):
@@ -733,9 +746,9 @@
 
     prepare(0)
     with jax.named_scope('w_f2'):
-        wait_faces(2)
+        wait_faces(0)
     for side, layer in ((0, 0), (1, 7)):
-        residual[layer] = -free[layer] * (ends[side] + halo[2, side])
+        residual[layer] = -free[layer] * (ends[side] + halo[0, side])
         rho[layer] = residual[layer]
         vectors[0, layer] = inverse[layer] * residual[layer]
 
@@ -746,7 +759,7 @@
         sums[key] = value if key not in sums else sums[key] + value
 
     for turn in range(ITERS):
-        phase = 3 + turn
+        phase = 1 + turn
         low = vectors[turn, 0]
         high = vectors[turn, 7]
         outer = {}
@@ -778,6 +791,7 @@
             rho[layer] = images[turn, layer] - SHIFTS[turn] * rho[layer]
             vectors[turn + 1, layer] = inverse[layer] * rho[layer]
         prepare(turn + 1)
+        serve_rest(WINDOWS[turn])
         with jax.named_scope('w_fc'):
             wait_faces(phase)
         for side, layer in ((0, 0), (1, 7)):
@@ -795,20 +809,37 @@
     for step in range(1, n):
         dot_copy(step).start()
     all_dots[slab] = dots[...]
+    for shift in range(-REACH, REACH + 1):
+
+        @pl.when(inside(slab + shift))
+        def _():
+            with jax.named_scope('w_rest'):
+                reply(shift, 1).wait_recv()
+
+    values = values + [gather_field(field) for field in range(1, fields)]
+    for row in range(height):
+        interface_ref[:, row * lanes : (row + 1) * lanes] = jnp.concatenate(
+            [value[row : row + 1] for value in values], 0
+        )
+    stores[0].start()
     for layer in range(1, 7):
         images[ITERS - 1, layer] = free[layer] * plane_sum(images[ITERS - 1, layer])
     with jax.named_scope('w_fc'):
-        wait_faces(3 + ITERS - 1)
+        wait_faces(ITERS)
     for side, layer in ((0, 0), (1, 7)):
         images[ITERS - 1, layer] = free[layer] * (
-            images[ITERS - 1, layer] + halo[3 + ITERS - 1, side]
+            images[ITERS - 1, layer] + halo[ITERS, side]
         )
     with jax.named_scope('w_dots'):
         for step in range(1, n):
             dot_copy(step).wait_recv()
-    total = jnp.sum(all_dots[...], axis=0)
-    found = {key: total[:, at : at + 1] for at, key in enumerate(keys)}
-    steps_taken = solve(found)
+    with jax.named_scope('solve'):
+        total = jnp.sum(all_dots[...], axis=0)
+        found = {
+            key: jnp.broadcast_to(total[:, at : at + 1], (8, elems))
+            for at, key in enumerate(keys)
+        }
+        steps_taken = solve(found)
     for layer in range(8):
         moved = boundary[layer]
         for turn in range(ITERS):
@@ -843,10 +874,12 @@
 
         @pl.when(inside(slab - shift))
         def _():
-            reply(shift).wait_send()
-
-    for store in stores:
-        store.wait()
+            reply(shift, 0).wait_send()
+            reply(shift, 1).wait_send()
+
+    with jax.named_scope('w_store'):
+        for store in stores:
+            store.wait()
 
 
 def flush(*refs):
@@ -869,7 +902,7 @@
     lanes = 128
     count = receptors // lanes
     cube = (8, 8, 8, elems)
-    phases = 3 + ITERS
+    phases = 1 + ITERS
     room = count // 2
     vmem = pl.BlockSpec(memory_space=pltpu.VMEM)
     hbm = pl.BlockSpec(memory_space=pltpu.HBM)
@@ -915,10 +948,12 @@
             pltpu.VMEM(cube, jnp.float32),
             pltpu.VMEM((2, 8, elems), jnp.float32),
             pltpu.VMEM((4, 8, elems), jnp.float32),
-            pltpu.VMEM((2,) + geometry.shape, jnp.float32),
+            pltpu.VMEM((2, 8, elems), jnp.float32),
+            pltpu.VMEM((8, elems), jnp.float32),
         ]
         + [pltpu.VMEM(cube, jnp.float32)] * 4
-        + [pltpu.SemaphoreType.DMA((slots,))] * 4
+        + [pltpu.SemaphoreType.DMA((slots,))] * 2
+        + [pltpu.SemaphoreType.DMA((2, slots))] * 2
         + [pltpu.SemaphoreType.DMA((phases, 2))] * 2
         + [pltpu.SemaphoreType.DMA((n,))] * 2
         + [pltpu.SemaphoreType.DMA((4,))] * 2

time: 41.2 us -> 35.3 us (0.86)
  Pallas kernels: 40.4 us -> 34.4 us
    pallas_call x1, Pallas kernels: 38.6 us -> 32.5 us  [body(): pl.pallas_call(functools.partial(kernel, n), out_shape=shapes, in_specs=[...]
where the time goes in v3:
time: 35.3 us; the launch traced here: 35.2 us
  Pallas kernels  34.4 us (97%)
  between operations  0.8 us (2%)
    pallas_call x1, Pallas kernels, body(): pl.pallas_call(functools.partial(kernel, n), out_shape=shapes, in_specs=[...  32.5 us
    pallas_call x1, Pallas kernels, body(): pl.pallas_call(flush, out_shape=shapes, in_specs=[vmem] * 3, out_specs=(h...  1.86 us

profile of v3, /device:TPU:0, one launch (start us, length us, event | category | flops | bytes accessed | tf_op | source)
XLA Modules:
  0.0 35.2 jit_solution(12682586322192180066)
XLA Ops:
  0.6 32.5 %shard_map.94 = (f32[8,8,8,128]{3,2,1,0:T(8,128)}, f32[8,8,8,128]{3,2,1,0:T(8,128)}, f32[5,2048]{1,0:T(8,128)}) custom-call(f32[5,512,128]{2,1,0:T(8,128)} %donor_hbm.1, f32[3,8,2048]{2,1,0:T(8,128)} %weights_hbm.1, s32[16,128]{1,0:T(8,128)} %bitcast.6, s32[16,128]{1,0:T(8,128)} %bitcast.7, f32[4,128]{1,0:T(4,128)} %geometry_hbm.1, s32[2,8]{1,0:T(2,128)} %wall_hbm.1, ...), custom_call_target="tpu_custom_call" | custom-call | tf_op jit(solution)/shard_map/pallas_call | solution.py:914
  33.2 1.9 %shard_map.95 = (f32[8,8,8,128]{3,2,1,0:T(8,128)}, f32[8,8,8,128]{3,2,1,0:T(8,128)}, f32[5,2048]{1,0:T(8,128)}) custom-call(f32[8,8,8,128]{3,2,1,0:T(8,128)} %get-tuple-element.9.refs_0_, f32[8,8,8,128]{3,2,1,0:T(8,128)} %get-tuple-element.10.refs_1_, f32[5,2048]{1,0:T(8,128)} %get-tuple-element.11.refs_2_), custom_call_target="tpu_custom_call" | custom-call | tf_op jit(solution)/shard_map/pallas_call | solution.py:974

commit v4 on v3

--- a/solution.py
+++ b/solution.py
@@ -119,16 +119,12 @@
     free,
     sharing,
     boundary,
-    ask_send,
-    ask_recv,
-    reply_send,
-    reply_recv,
+    ask_sem,
+    reply_sem,
     face_send,
     face_recv,
-    dot_send,
-    dot_recv,
-    rim_send,
-    rim_recv,
+    dot_sem,
+    rim_sem,
     geometry_send,
     geometry_recv,
     store_sem,
@@ -253,8 +249,8 @@
         return pltpu.make_async_remote_copy(
             src_ref=request_ref.at[shift + REACH],
             dst_ref=asked.at[shift + REACH],
-            send_sem=ask_send.at[shift + REACH],
-            recv_sem=ask_recv.at[shift + REACH],
+            send_sem=ask_sem.at[0],
+            recv_sem=ask_sem.at[1 if shift == 0 else 2],
             device_id=(other, lax.rem(slab + shift + n, n)),
             device_id_type=MESH,
         )
@@ -264,19 +260,51 @@
         return pltpu.make_async_remote_copy(
             src_ref=answer.at[shift + REACH, span],
             dst_ref=answered.at[shift + REACH, span],
-            send_sem=reply_send.at[part, shift + REACH],
-            recv_sem=reply_recv.at[part, shift + REACH],
+            send_sem=reply_sem.at[0, part],
+            recv_sem=reply_sem.at[1, part],
             device_id=(other, lax.rem(slab - shift + n, n)),
             device_id_type=MESH,
         )
+
+    def asks(many, sem):
+        return pltpu.make_async_remote_copy(
+            src_ref=asked.at[pl.ds(0, many)],
+            dst_ref=asked.at[pl.ds(0, many)],
+            send_sem=ask_sem.at[0],
+            recv_sem=ask_sem.at[sem],
+            device_id=(other, slab),
+            device_id_type=MESH,
+        )
+
+    def replies(many, part):
+        span = pl.ds(0, 1) if part == 0 else pl.ds(1, fields - 1)
+        return pltpu.make_async_remote_copy(
+            src_ref=answered.at[pl.ds(0, many), span],
+            dst_ref=answered.at[pl.ds(0, many), span],
+            send_sem=reply_sem.at[0, part],
+            recv_sem=reply_sem.at[1, part],
+            device_id=(other, slab),
+            device_id_type=MESH,
+        )
+
+    partners = 0
+    for shift in range(-REACH, REACH + 1):
+        partners = partners + jnp.where(inside(slab + shift), 1, 0)
+
+    def with_partners(action):
+        for many in range(REACH + 1, slots + 1):
+
+            @pl.when(partners == many)
+            def _():
+                action(many)
 
     def face_copy(phase, up):
         step = 1 if up else n - 1
         return pltpu.make_async_remote_copy(
             src_ref=faces.at[phase, 1 if up else 0],
             dst_ref=halo.at[phase, 0 if up else 1],
-            send_sem=face_send.at[phase, 1 if up else 0],
-            recv_sem=face_recv.at[phase, 0 if up else 1],
+            send_sem=face_send.at[1 if up else 0],
+            recv_sem=face_recv.at[phase % 2, 0 if up else 1],
             device_id=(mesh_id, lax.rem(slab + step, n)),
             device_id_type=MESH,
         )
@@ -311,9 +339,19 @@
         return pltpu.make_async_remote_copy(
             src_ref=dots,
             dst_ref=all_dots.at[slab],
-            send_sem=dot_send.at[step],
-            recv_sem=dot_recv.at[step],
+            send_sem=dot_sem.at[0],
+            recv_sem=dot_sem.at[1],
             device_id=(mesh_id, lax.rem(slab + step, n)),
+            device_id_type=MESH,
+        )
+
+    def all_dot_copies():
+        return pltpu.make_async_remote_copy(
+            src_ref=all_dots.at[pl.ds(0, n - 1)],
+            dst_ref=all_dots.at[pl.ds(0, n - 1)],
+            send_sem=dot_sem.at[0],
+            recv_sem=dot_sem.at[1],
+            device_id=(mesh_id, lax.rem(slab + 1, n)),
             device_id_type=MESH,
         )
 
@@ -326,9 +364,19 @@
         return pltpu.make_async_remote_copy(
             src_ref=rim.at[1 - at % 2],
             dst_ref=rim_halo.at[at],
-            send_sem=rim_send.at[at],
-            recv_sem=rim_recv.at[at],
+            send_sem=rim_sem.at[0],
+            recv_sem=rim_sem.at[1],
             device_id=(mesh_id, lax.rem(slab + rim_jumps[at] + n, n)),
+            device_id_type=MESH,
+        )
+
+    def rims(many):
+        return pltpu.make_async_remote_copy(
+            src_ref=rim_halo.at[pl.ds(0, many)],
+            dst_ref=rim_halo.at[pl.ds(0, many)],
+            send_sem=rim_sem.at[0],
+            recv_sem=rim_sem.at[1],
+            device_id=(mesh_id, lax.rem(slab + 1, n)),
             device_id_type=MESH,
         )
 
@@ -359,6 +407,16 @@
 
     phases = halo.shape[0]
     blank = jnp.zeros(halo.shape[2:], jnp.float32)
+
+    for shift in range(-REACH, REACH + 1):
+
+        @pl.when(jnp.logical_not(inside(slab + shift)))
+        def _():
+            answered[shift + REACH] = jnp.zeros(answered.shape[1:], jnp.float32)
+
+        @pl.when(jnp.logical_not(inside(slab - shift)))
+        def _():
+            asked[shift + REACH] = jnp.zeros(asked.shape[1:], jnp.float32)
 
     for at in range(4):
 
@@ -542,26 +600,26 @@
                         :, t * lanes : (t + 1) * lanes
                     ]
 
-    def serve(turn, carry):
-        shift = ((turn + 1) // 2) * (2 * (turn % 2) - 1)
+    near_first = [0] + [sign * reach for reach in range(1, REACH + 1) for sign in (1, -1)]
+    with jax.named_scope('w_ask'):
+        asks(1, 1).wait_recv()
+    evaluate(0, 0, 1)
+    reply(0, 0).start()
+    with jax.named_scope('w_ask'):
+        with_partners(lambda many: asks(many - 1, 2).wait_recv())
+    for shift in near_first[1:]:
+        evaluate(shift, 0, 1)
+    for shift in near_first[1:]:
 
         @pl.when(inside(slab - shift))
         def _():
-            with jax.named_scope('w_ask'):
-                ask(shift).wait_recv()
-            evaluate(shift, 0, 1)
-            with jax.named_scope('reply'):
-                reply(shift, 0).start()
-
-        return carry
-
-    lax.fori_loop(0, slots, serve, 0)
+            reply(shift, 0).start()
+
     turns_left = list(range(slots))
 
     def serve_rest(many):
         for _ in range(many):
-            turn = turns_left.pop(0)
-            shift = ((turn + 1) // 2) * (2 * (turn % 2) - 1)
+            shift = near_first[turns_left.pop(0)]
 
             @pl.when(inside(slab - shift))
             def _():
@@ -581,16 +639,8 @@
         plans.append((first, second, offset, spots))
 
     serve_rest(2)
-    for shift in range(-REACH, REACH + 1):
-
-        @pl.when(jnp.logical_not(inside(slab + shift)))
-        def _():
-            answered[shift + REACH] = jnp.zeros(answered.shape[1:], jnp.float32)
-
-        @pl.when(inside(slab + shift))
-        def _():
-            with jax.named_scope('w_reply'):
-                reply(shift, 0).wait_recv()
+    with jax.named_scope('w_reply'):
+        with_partners(lambda many: replies(many, 0).wait_recv())
 
     def along_lanes(tile, index):
         return jnp.take_along_axis(tile, index, axis=1, mode="promise_in_bounds")
@@ -709,11 +759,7 @@
     serve_rest(1)
 
     with jax.named_scope('w_rim'):
-        for at in range(4):
-
-            @pl.when(rim_comes[at])
-            def _():
-                rim_copy(at).wait_recv()
+        with_partners(lambda many: rims(many - 1).wait_recv())
 
     low = spread_out(rim_halo[0]) * sharing[0]
     high = spread_out(rim_halo[1]) * sharing[7]
@@ -809,12 +855,8 @@
     for step in range(1, n):
         dot_copy(step).start()
     all_dots[slab] = dots[...]
-    for shift in range(-REACH, REACH + 1):
-
-        @pl.when(inside(slab + shift))
-        def _():
-            with jax.named_scope('w_rest'):
-                reply(shift, 1).wait_recv()
+    with jax.named_scope('w_rest'):
+        with_partners(lambda many: replies(many, 1).wait_recv())
 
     values = values + [gather_field(field) for field in range(1, fields)]
     for row in range(height):
@@ -831,8 +873,7 @@
             images[ITERS - 1, layer] + halo[ITERS, side]
         )
     with jax.named_scope('w_dots'):
-        for step in range(1, n):
-            dot_copy(step).wait_recv()
+        all_dot_copies().wait_recv()
     with jax.named_scope('solve'):
         total = jnp.sum(all_dots[...], axis=0)
         found = {
@@ -852,30 +893,17 @@
             left_over = left_over - steps_taken[turn] * images[turn, layer]
         rho[layer] = left_over
     stores[2].start()
-    for step in range(1, n):
-        dot_copy(step).wait_send()
+    all_dot_copies().wait_send()
     for side in range(2):
 
         @pl.when(near[1 - side])
         def _():
             geometry_copy(side == 0).wait_send()
 
-    for at in range(4):
-
-        @pl.when(rim_sends[at])
-        def _():
-            rim_copy(at).wait_send()
-
-    for shift in range(-REACH, REACH + 1):
-
-        @pl.when(inside(slab + shift))
-        def _():
-            ask(shift).wait_send()
-
-        @pl.when(inside(slab - shift))
-        def _():
-            reply(shift, 0).wait_send()
-            reply(shift, 1).wait_send()
+    with_partners(lambda many: rims(many - 1).wait_send())
+    with_partners(lambda many: asks(many, 1).wait_send())
+    for part in range(2):
+        with_partners(lambda many: replies(many, part).wait_send())
 
     with jax.named_scope('w_store'):
         for store in stores:
@@ -952,11 +980,10 @@
             pltpu.VMEM((8, elems), jnp.float32),
         ]
         + [pltpu.VMEM(cube, jnp.float32)] * 4
-        + [pltpu.SemaphoreType.DMA((slots,))] * 2
-        + [pltpu.SemaphoreType.DMA((2, slots))] * 2
-        + [pltpu.SemaphoreType.DMA((phases, 2))] * 2
-        + [pltpu.SemaphoreType.DMA((n,))] * 2
-        + [pltpu.SemaphoreType.DMA((4,))] * 2
+        + [pltpu.SemaphoreType.DMA((3,)), pltpu.SemaphoreType.DMA((2, 2))]
+        + [pltpu.SemaphoreType.DMA((2,)), pltpu.SemaphoreType.DMA((2, 2))]
+        + [pltpu.SemaphoreType.DMA((2,))]
+        + [pltpu.SemaphoreType.DMA((2,))]
         + [pltpu.SemaphoreType.DMA((2,))] * 2
         + [pltpu.SemaphoreType.DMA((3,))],
         compiler_params=pltpu.CompilerParams(

time: 35.3 us -> 35.1 us (level)
  no operation moved by 1% of the time
where the time goes in v4:
time: 35.1 us; the launch traced here: 35 us
  Pallas kernels  34.2 us (97%)
  between operations  0.8 us (2%)
    pallas_call x1, Pallas kernels, body(): pl.pallas_call(functools.partial(kernel, n), out_shape=shapes, in_specs=[...  32.3 us
    pallas_call x1, Pallas kernels, body(): pl.pallas_call(flush, out_shape=shapes, in_specs=[vmem] * 3, out_specs=(h...  1.86 us

profile of v4, /device:TPU:0, one launch (start us, length us, event | category | flops | bytes accessed | tf_op | source)
XLA Modules:
  0.0 35.0 jit_solution(7385867889362126485)
XLA Ops:
  0.6 32.3 %shard_map.94 = (f32[8,8,8,128]{3,2,1,0:T(8,128)}, f32[8,8,8,128]{3,2,1,0:T(8,128)}, f32[5,2048]{1,0:T(8,128)}) custom-call(f32[5,512,128]{2,1,0:T(8,128)} %donor_hbm.1, f32[3,8,2048]{2,1,0:T(8,128)} %weights_hbm.1, s32[16,128]{1,0:T(8,128)} %bitcast.6, s32[16,128]{1,0:T(8,128)} %bitcast.7, f32[4,128]{1,0:T(4,128)} %geometry_hbm.1, s32[2,8]{1,0:T(2,128)} %wall_hbm.1, ...), custom_call_target="tpu_custom_call" | custom-call | tf_op jit(solution)/shard_map/pallas_call | solution.py:942
  33.0 1.9 %shard_map.95 = (f32[8,8,8,128]{3,2,1,0:T(8,128)}, f32[8,8,8,128]{3,2,1,0:T(8,128)}, f32[5,2048]{1,0:T(8,128)}) custom-call(f32[8,8,8,128]{3,2,1,0:T(8,128)} %get-tuple-element.9.refs_0_, f32[8,8,8,128]{3,2,1,0:T(8,128)} %get-tuple-element.10.refs_1_, f32[5,2048]{1,0:T(8,128)} %get-tuple-element.11.refs_2_), custom_call_target="tpu_custom_call" | custom-call | tf_op jit(solution)/shard_map/pallas_call | solution.py:1001

commit v5 on v4

--- a/solution.py
+++ b/solution.py
@@ -79,12 +79,10 @@
     geometry_hbm,
     wall_hbm,
     forcing_hbm,
-    velocity_hbm,
-    residual_hbm,
-    interface_hbm,
     velocity,
+    residual_out,
+    interface_ref,
     residual,
-    interface_ref,
     donor_ref,
     forcing_ref,
     weights_ref,
@@ -127,7 +125,6 @@
     rim_sem,
     geometry_send,
     geometry_recv,
-    store_sem,
 ):
     points, derivative, quad = gll_tables()
     stiff = (derivative.T * quad) @ derivative / quad[:, None]
@@ -390,13 +387,6 @@
             device_id=(mesh_id, lax.rem(slab + (1 if up else n - 1), n)),
             device_id_type=MESH,
         )
-
-    stores = [
-        pltpu.make_async_copy(source, target, store_sem.at[at])
-        for at, (source, target) in enumerate(
-            ((interface_ref, interface_hbm), (velocity, velocity_hbm), (rho, residual_hbm))
-        )
-    ]
 
     for distance in range(REACH + 1):
         for shift in sorted({distance, -distance}):
@@ -863,7 +853,6 @@
         interface_ref[:, row * lanes : (row + 1) * lanes] = jnp.concatenate(
             [value[row : row + 1] for value in values], 0
         )
-    stores[0].start()
     for layer in range(1, 7):
         images[ITERS - 1, layer] = free[layer] * plane_sum(images[ITERS - 1, layer])
     with jax.named_scope('w_fc'):
@@ -886,13 +875,11 @@
         for turn in range(ITERS):
             moved = moved + steps_taken[turn] * vectors[turn, layer]
         velocity[layer] = moved
-    stores[1].start()
     for layer in range(8):
         left_over = residual[layer]
         for turn in range(ITERS):
             left_over = left_over - steps_taken[turn] * images[turn, layer]
-        rho[layer] = left_over
-    stores[2].start()
+        residual_out[layer] = left_over
     all_dot_copies().wait_send()
     for side in range(2):
 
@@ -904,10 +891,6 @@
     with_partners(lambda many: asks(many, 1).wait_send())
     for part in range(2):
         with_partners(lambda many: replies(many, part).wait_send())
-
-    with jax.named_scope('w_store'):
-        for store in stores:
-            store.wait()
 
 
 def flush(*refs):
@@ -943,11 +926,9 @@
         functools.partial(kernel, n),
         out_shape=shapes,
         in_specs=[hbm] * 7,
-        out_specs=(hbm, hbm, hbm),
+        out_specs=(vmem, vmem, vmem),
         scratch_shapes=[
             pltpu.VMEM(cube, jnp.float32),
-            pltpu.VMEM(cube, jnp.float32),
-            pltpu.VMEM((fields, receptors), jnp.float32),
             pltpu.VMEM((fields, 512, elems), jnp.float32),
             pltpu.VMEM(cube, jnp.float32),
             pltpu.VMEM(interp_weights.shape, jnp.float32),
@@ -984,19 +965,23 @@
         + [pltpu.SemaphoreType.DMA((2,)), pltpu.SemaphoreType.DMA((2, 2))]
         + [pltpu.SemaphoreType.DMA((2,))]
         + [pltpu.SemaphoreType.DMA((2,))]
-        + [pltpu.SemaphoreType.DMA((2,))] * 2
-        + [pltpu.SemaphoreType.DMA((3,))],
+        + [pltpu.SemaphoreType.DMA((2,))] * 2,
         compiler_params=pltpu.CompilerParams(
-            collective_id=0, has_side_effects=True, vmem_limit_bytes=67043328
+            collective_id=0, has_side_effects=True, vmem_limit_bytes=48 * 1024 * 1024
         ),
     )(
-        donor_fields,
-        interp_weights,
-        donor_owner.reshape(count, lanes),
-        donor_element.reshape(count, lanes),
-        geometry,
-        wall_flag,
-        forcing.reshape(cube),
+        *[
+            pltpu.with_memory_space_constraint(array, pltpu.HBM)
+            for array in (
+                donor_fields,
+                interp_weights,
+                donor_owner.reshape(count, lanes),
+                donor_element.reshape(count, lanes),
+                geometry,
+                wall_flag,
+                forcing.reshape(cube),
+            )
+        ]
     )
     velocity, residual, interface = pl.pallas_call(
         flush,
@@ -1004,6 +989,7 @@
         in_specs=[vmem] * 3,
         out_specs=(hbm,) * 3,
         scratch_shapes=[pltpu.SemaphoreType.DMA((3,))],
+        compiler_params=pltpu.CompilerParams(vmem_limit_bytes=1024 * 1024),
     )(*outputs)
     return (velocity.reshape(512, elems), residual.reshape(512, elems), interface)
 

time: 35.1 us -> 33.4 us (0.952)
  Pallas kernels: 34.2 us -> 32.4 us
    pallas_call x1, Pallas kernels: 1.86 us -> 0.83 us  [body(): pl.pallas_call(flush, out_shape=shapes, in_specs=[vmem] * 3, out_specs=(h...]
    pallas_call x1, Pallas kernels: 32.3 us -> 31.6 us  [body(): pl.pallas_call(functools.partial(kernel, n), out_shape=shapes, in_specs=[...]
where the time goes in v5:
time: 33.4 us; the launch traced here: 33.2 us
  Pallas kernels  32.4 us (97%)
  between operations  0.8 us (2%)
    pallas_call x1, Pallas kernels, body(): pl.pallas_call(functools.partial(kernel, n), out_shape=shapes, in_specs=[...  31.6 us
    pallas_call x1, Pallas kernels, body(): pl.pallas_call(flush, out_shape=shapes, in_specs=[vmem] * 3, out_specs=(h...  0.83 us

profile of v5, /device:TPU:0, one launch (start us, length us, event | category | flops | bytes accessed | tf_op | source)
XLA Modules:
  0.0 33.2 jit_solution(2162711724672692600)
XLA Ops:
  0.6 31.6 %shard_map.94 = (f32[8,8,8,128]{3,2,1,0:T(8,128)S(1)}, f32[8,8,8,128]{3,2,1,0:T(8,128)S(1)}, f32[5,2048]{1,0:T(8,128)S(1)}) custom-call(f32[5,512,128]{2,1,0:T(8,128)} %donor_hbm.1, f32[3,8,2048]{2,1,0:T(8,128)} %weights_hbm.1, s32[16,128]{1,0:T(8,128)} %bitcast.6, s32[16,128]{1,0:T(8,128)} %bitcast.7, f32[4,128]{1,0:T(4,128)} %geometry_hbm.1, ...), custom_call_target="tpu_custom_call" | custom-call | tf_op jit(solution)/shard_map/pallas_call | solution.py:925
  32.2 0.8 %shard_map.95 = (f32[8,8,8,128]{3,2,1,0:T(8,128)}, f32[8,8,8,128]{3,2,1,0:T(8,128)}, f32[5,2048]{1,0:T(8,128)}) custom-call(f32[8,8,8,128]{3,2,1,0:T(8,128)S(1)} %get-tuple-element.9.refs_0_, f32[8,8,8,128]{3,2,1,0:T(8,128)S(1)} %get-tuple-element.10.refs_1_, f32[5,2048]{1,0:T(8,128)S(1)} %get-tuple-element.11.refs_2_), custom_call_target="tpu_custom_call" | custom-call | tf_op jit(solution)/shard_map/pallas_call | solution.py:986

commit v6 on v5

--- a/solution.py
+++ b/solution.py
@@ -15,7 +15,7 @@
 CHUNK = 256
 ORDER = (0, 7, 1, 2, 3, 4, 5, 6)
 SHIFTS = (1.5, 0.5)
-WINDOWS = (1, 1)
+WINDOW = 2
 MESH = pl.DeviceIdType.MESH
 
 
@@ -113,6 +113,8 @@
     rim_halo,
     geometry_halo,
     packet,
+    far_faces,
+    far_halo,
     inverse,
     free,
     sharing,
@@ -121,6 +123,7 @@
     reply_sem,
     face_send,
     face_recv,
+    far_sem,
     dot_sem,
     rim_sem,
     geometry_send,
@@ -300,8 +303,8 @@
         return pltpu.make_async_remote_copy(
             src_ref=faces.at[phase, 1 if up else 0],
             dst_ref=halo.at[phase, 0 if up else 1],
-            send_sem=face_send.at[1 if up else 0],
-            recv_sem=face_recv.at[phase % 2, 0 if up else 1],
+            send_sem=face_send.at[phase % 3, 1 if up else 0],
+            recv_sem=face_recv.at[phase % 3, 0 if up else 1],
             device_id=(mesh_id, lax.rem(slab + step, n)),
             device_id_type=MESH,
         )
@@ -341,6 +344,46 @@
             device_id=(mesh_id, lax.rem(slab + step, n)),
             device_id_type=MESH,
         )
+
+    def far_copy(up):
+        side = 0 if up else 1
+        return pltpu.make_async_remote_copy(
+            src_ref=far_faces.at[1 - side],
+            dst_ref=far_halo.at[side],
+            send_sem=far_sem.at[0, side],
+            recv_sem=far_sem.at[1, side],
+            device_id=(mesh_id, lax.rem(slab + (2 if up else n - 2), n)),
+            device_id_type=MESH,
+        )
+
+    above_far = slab < n - 2
+    below_far = slab > 1
+
+    def send_far():
+        @pl.when(above_far)
+        def _():
+            far_copy(True).start()
+
+        @pl.when(below_far)
+        def _():
+            far_copy(False).start()
+
+    def wait_far():
+        @pl.when(below_far)
+        def _():
+            far_copy(True).wait_recv()
+
+        @pl.when(above_far)
+        def _():
+            far_copy(False).wait_recv()
+
+        @pl.when(above_far)
+        def _():
+            far_copy(True).wait_send()
+
+        @pl.when(below_far)
+        def _():
+            far_copy(False).wait_send()
 
     def all_dot_copies():
         return pltpu.make_async_remote_copy(
@@ -419,6 +462,14 @@
         @pl.when(jnp.logical_not(near[side]))
         def _():
             geometry_halo[side] = jnp.zeros(geometry_halo.shape[1:], jnp.float32)
+
+    @pl.when(jnp.logical_not(below_far))
+    def _():
+        far_halo[0] = blank
+
+    @pl.when(jnp.logical_not(above_far))
+    def _():
+        far_halo[1] = blank
 
     @pl.when(slab == 0)
     def _():
@@ -768,17 +819,19 @@
         more = more + term + across_z * (spread_out(rim_halo[2 + side]) * half_share)
         ends.append(residual[layer] + plane_sum(edge * more))
 
-    def prepare(turn):
-        def read(k):
-            return vectors[turn, k]
-
+    def prepare_outer(turn):
+        for layer in (0, 7):
+            partial[layer] = g_z * inner_z(lambda k: vectors[turn, k], layer)
+
+    def prepare_inner(turn):
         for layer in range(1, 7):
             tile = vectors[turn, layer]
-            partial[layer] = (
-                in_plane(tile, here) + g_m * tile + g_z * inner_z(read, layer)
-            )
-        for layer in (0, 7):
-            partial[layer] = g_z * inner_z(read, layer)
+            along_z = inner_z(lambda k: vectors[turn, k], layer)
+            partial[layer] = in_plane(tile, here) + g_m * tile + g_z * along_z
+
+    def prepare(turn):
+        prepare_outer(turn)
+        prepare_inner(turn)
 
     prepare(0)
     with jax.named_scope('w_f2'):
@@ -794,46 +847,78 @@
         value = jnp.sum(value, axis=0)
         sums[key] = value if key not in sums else sums[key] + value
 
-    for turn in range(ITERS):
-        phase = 1 + turn
+    def outer_tiles(turn):
         low = vectors[turn, 0]
         high = vectors[turn, 7]
-        outer = {}
+        tiles = {}
         for layer in (0, 7):
             tile = vectors[turn, layer]
             total = in_plane(tile, here) + g_m * tile + g_z * outer_z(low, high, layer)
-            outer[layer] = edge * (total + partial[layer])
-            images[turn, layer] = plane_sum(outer[layer])
-        faces[phase, 0] = images[turn, 0]
-        faces[phase, 1] = images[turn, 7]
-        send_faces(phase)
-        last = turn == ITERS - 1
+            tiles[layer] = edge * (total + partial[layer])
+            images[turn, layer] = plane_sum(tiles[layer])
+        return tiles
+
+    def inner_tiles(turn, tiles):
+        low = vectors[turn, 0]
+        high = vectors[turn, 7]
         for layer in range(8):
-            if layer in outer:
-                tile = outer[layer]
+            if layer in tiles:
+                tile = tiles[layer]
             else:
                 tile = partial[layer] + g_z * outer_z(low, high, layer)
                 tile = weights(layer) * tile
             for other_turn in range(turn + 1):
                 gather_sum((other_turn, turn), tile * vectors[other_turn, layer])
-            gather_sum(
-                turn, vectors[turn, layer] * residual[layer] * sharing[layer]
-            )
-            if layer not in outer:
+            gather_sum(turn, vectors[turn, layer] * residual[layer] * sharing[layer])
+            if layer not in tiles:
+                last = turn == ITERS - 1
                 images[turn, layer] = tile if last else free[layer] * plane_sum(tile)
-        if last:
-            break
-        for layer in range(1, 7):
+
+    def advance(turn, layers):
+        for layer in layers:
             rho[layer] = images[turn, layer] - SHIFTS[turn] * rho[layer]
             vectors[turn + 1, layer] = inverse[layer] * rho[layer]
-        prepare(turn + 1)
-        serve_rest(WINDOWS[turn])
-        with jax.named_scope('w_fc'):
-            wait_faces(phase)
-        for side, layer in ((0, 0), (1, 7)):
-            images[turn, layer] = free[layer] * (images[turn, layer] + halo[phase, side])
-            rho[layer] = images[turn, layer] - SHIFTS[turn] * rho[layer]
-            vectors[turn + 1, layer] = inverse[layer] * rho[layer]
+
+    sides = ((0, 0), (1, 7))
+    tiles = outer_tiles(0)
+    guesses = []
+    for side, layer in sides:
+        faces[1, side] = images[0, layer]
+        far_faces[side] = inverse[layer] * images[0, layer]
+    send_faces(1)
+    send_far()
+    for side, layer in sides:
+        guesses.append(inverse[layer] * (images[0, layer] - SHIFTS[0] * rho[layer]))
+    inner_tiles(0, tiles)
+    advance(0, range(1, 7))
+    prepare_outer(1)
+    for side, layer in sides:
+        faces[2, side] = partial[layer] + g_z * (guesses[1 - side] * float(stiff[0, 7]))
+    send_faces(2)
+    prepare_inner(1)
+    serve_rest(WINDOW)
+    with jax.named_scope('w_fc'):
+        wait_faces(1)
+        wait_far()
+        wait_faces(2)
+    for side, layer in sides:
+        images[0, layer] = free[layer] * (images[0, layer] + halo[1, side])
+    advance(0, (0, 7))
+    tiles = outer_tiles(1)
+    for side, layer in sides:
+        along = [geometry_halo[side, d : d + 1, :] for d in range(4)]
+        own = vectors[1, layer]
+        term = in_plane(own, along) + (along[2] * float(stiff[0, 0]) + along[3]) * own
+        term = term + halo[2, side] + (along[2] * float(stiff[0, 7])) * far_halo[side]
+        images[1, layer] = free[layer] * (images[1, layer] + plane_sum(edge * term))
+    inner_tiles(1, tiles)
+    advance(1, range(8))
+    prepare(2)
+    tiles = outer_tiles(2)
+    for side, layer in sides:
+        faces[ITERS, side] = images[2, layer]
+    send_faces(ITERS)
+    inner_tiles(2, tiles)
 
     keys = list(range(ITERS)) + [(a, b) for b in range(ITERS) for a in range(b + 1)]
     spot = lax.broadcasted_iota(jnp.int32, (1, 128), 1)
@@ -959,10 +1044,13 @@
             pltpu.VMEM((4, 8, elems), jnp.float32),
             pltpu.VMEM((2, 8, elems), jnp.float32),
             pltpu.VMEM((8, elems), jnp.float32),
+            pltpu.VMEM((2, 8, 8, elems), jnp.float32),
+            pltpu.VMEM((2, 8, 8, elems), jnp.float32),
         ]
         + [pltpu.VMEM(cube, jnp.float32)] * 4
         + [pltpu.SemaphoreType.DMA((3,)), pltpu.SemaphoreType.DMA((2, 2))]
-        + [pltpu.SemaphoreType.DMA((2,)), pltpu.SemaphoreType.DMA((2, 2))]
+        + [pltpu.SemaphoreType.DMA((3, 2))] * 2
+        + [pltpu.SemaphoreType.DMA((2, 2))]
         + [pltpu.SemaphoreType.DMA((2,))]
         + [pltpu.SemaphoreType.DMA((2,))]
         + [pltpu.SemaphoreType.DMA((2,))] * 2,

time: 33.4 us -> 30.8 us (0.922)
  Pallas kernels: 32.4 us -> 29.8 us
    pallas_call x1, Pallas kernels: 31.6 us -> 29 us  [body(): pl.pallas_call(functools.partial(kernel, n), out_shape=shapes, in_specs=[...]
where the time goes in v6:
time: 30.8 us; the launch traced here: 30.6 us
  Pallas kernels  29.8 us (97%)
  between operations  0.8 us (3%)
    pallas_call x1, Pallas kernels, body(): pl.pallas_call(functools.partial(kernel, n), out_shape=shapes, in_specs=[...  29 us
    pallas_call x1, Pallas kernels, body(): pl.pallas_call(flush, out_shape=shapes, in_specs=[vmem] * 3, out_specs=(h...  0.83 us

profile of v6, /device:TPU:0, one launch (start us, length us, event | category | flops | bytes accessed | tf_op | source)
XLA Modules:
  0.0 30.6 jit_solution(5835847876345702185)
XLA Ops:
  0.6 29.0 %shard_map.94 = (f32[8,8,8,128]{3,2,1,0:T(8,128)S(1)}, f32[8,8,8,128]{3,2,1,0:T(8,128)S(1)}, f32[5,2048]{1,0:T(8,128)S(1)}) custom-call(f32[5,512,128]{2,1,0:T(8,128)} %donor_hbm.1, f32[3,8,2048]{2,1,0:T(8,128)} %weights_hbm.1, s32[16,128]{1,0:T(8,128)} %bitcast.6, s32[16,128]{1,0:T(8,128)} %bitcast.7, f32[4,128]{1,0:T(4,128)} %geometry_hbm.1, ...), custom_call_target="tpu_custom_call" | custom-call | tf_op jit(solution)/shard_map/pallas_call | solution.py:1010
  29.6 0.8 %shard_map.95 = (f32[8,8,8,128]{3,2,1,0:T(8,128)}, f32[8,8,8,128]{3,2,1,0:T(8,128)}, f32[5,2048]{1,0:T(8,128)}) custom-call(f32[8,8,8,128]{3,2,1,0:T(8,128)S(1)} %get-tuple-element.9.refs_0_, f32[8,8,8,128]{3,2,1,0:T(8,128)S(1)} %get-tuple-element.10.refs_1_, f32[5,2048]{1,0:T(8,128)S(1)} %get-tuple-element.11.refs_2_), custom_call_target="tpu_custom_call" | custom-call | tf_op jit(solution)/shard_map/pallas_call | solution.py:1074

commit v7 on v6

--- a/solution.py
+++ b/solution.py
@@ -718,11 +718,16 @@
     spot = lax.broadcasted_iota(jnp.int32, (groups * height, elems), 1)
     piece = row % height
     target = (groups * (piece % per_side) + row // height) * EX + (EX - 1) * (piece // per_side)
+    pieces = []
+    rest = rows
+    for _ in range(3):
+        piece = rest.astype(jnp.bfloat16)
+        pieces.append(piece)
+        rest = rest - piece.astype(jnp.float32)
     placed = lax.dot_general(
-        rows,
-        flag(spot == target),
+        jnp.concatenate(pieces, 0),
+        jnp.concatenate([flag(spot == target).astype(jnp.bfloat16)] * 3, 0),
         (((0,), (0,)), ((), ())),
-        precision=lax.Precision.HIGHEST,
         preferred_element_type=jnp.float32,
     ).reshape(8, 8, elems)
     rim[0] = placed[0]

time: 30.8 us -> 30.7 us (level)
  no operation moved by 1% of the time
where the time goes in v7:
time: 30.7 us; the launch traced here: 30.6 us
  Pallas kernels  29.8 us (97%)
  between operations  0.8 us (3%)
    pallas_call x1, Pallas kernels, body(): pl.pallas_call(functools.partial(kernel, n), out_shape=shapes, in_specs=[...  28.9 us
    pallas_call x1, Pallas kernels, body(): pl.pallas_call(flush, out_shape=shapes, in_specs=[vmem] * 3, out_specs=(h...  0.83 us

profile of v7, /device:TPU:0, one launch (start us, length us, event | category | flops | bytes accessed | tf_op | source)
XLA Modules:
  0.0 30.6 jit_solution(16719898960998409493)
XLA Ops:
  0.6 28.9 %shard_map.94 = (f32[8,8,8,128]{3,2,1,0:T(8,128)S(1)}, f32[8,8,8,128]{3,2,1,0:T(8,128)S(1)}, f32[5,2048]{1,0:T(8,128)S(1)}) custom-call(f32[5,512,128]{2,1,0:T(8,128)} %donor_hbm.1, f32[3,8,2048]{2,1,0:T(8,128)} %weights_hbm.1, s32[16,128]{1,0:T(8,128)} %bitcast.6, s32[16,128]{1,0:T(8,128)} %bitcast.7, f32[4,128]{1,0:T(4,128)} %geometry_hbm.1, ...), custom_call_target="tpu_custom_call" | custom-call | tf_op jit(solution)/shard_map/pallas_call | solution.py:1015
  29.6 0.8 %shard_map.95 = (f32[8,8,8,128]{3,2,1,0:T(8,128)}, f32[8,8,8,128]{3,2,1,0:T(8,128)}, f32[5,2048]{1,0:T(8,128)}) custom-call(f32[8,8,8,128]{3,2,1,0:T(8,128)S(1)} %get-tuple-element.9.refs_0_, f32[8,8,8,128]{3,2,1,0:T(8,128)S(1)} %get-tuple-element.10.refs_1_, f32[5,2048]{1,0:T(8,128)S(1)} %get-tuple-element.11.refs_2_), custom_call_target="tpu_custom_call" | custom-call | tf_op jit(solution)/shard_map/pallas_call | solution.py:1079
